TPU v7x, 256 devices: a whole 4x4x8 slice. The times are simulated.
256 devices in a mesh: seq: 32 (over y_lo, z, core), head: 8 (over x, y_hi).
Axes of the slice: x: 4, y: 4 (y_hi: 2, y_lo: 2; y = y_hi * 2 + y_lo), z: 8, core: 2. Of those that a mesh axis runs over, the one named last changes fastest.
Arguments:
- queries: bfloat16 [4, 64, 64, 128], P(None, None, 'head'), may hold values from -15 to 15
- new_keys: bfloat16 [4, 64, 8, 128], P(None, None, 'head'), may hold values from -16 to 16
- new_values: bfloat16 [4, 64, 8, 128], P(None, None, 'head'), may hold values from -6 to 6
- cache_keys: bfloat16 [4, 65536, 8, 128], P(None, 'seq', 'head'), may hold values from -6 to 6
- cache_values: bfloat16 [4, 65536, 8, 128], P(None, 'seq', 'head'), may hold values from -6 to 6
- parents: int32 [4, 64], replicated, may hold values from 0 to 63, as said below
- kv_lengths: int32 [4], replicated, may hold values from 1 to 65536
- out_weight: bfloat16 [8192, 8192], P('head', 'seq'), may hold values from -0.5 to 0.5
Outputs:
- mixed: bfloat16 [256, 8192], P('head', 'seq')
Inputs may be any that keep to these rules, and one draw needn't show every extreme that they name: parents[r, 0] = 0 for the root; for i >= 1, parents[r, i] < i.
All inputs are finite; a program needn't handle non-finite values.
Results may differ from a plain program's by a relative error of at most 0.0045.
Values may be sent and summed in bfloat16 or wider, within the bound.
No kernel may reach another device: no remote copies, remote signals or barrier semaphores. Data moves between devices by JAX's collectives and lax.ppermute only.
A program may use at most 64 MiB of HBM per device.

v0:
```python
import math

import jax
import jax.numpy as jnp
from jax import lax
from jax.sharding import PartitionSpec as P

lowest = -1e30


def from_everyone(array, axis):
    peers = lax.axis_size(axis)
    return lax.all_to_all(
        jnp.broadcast_to(array[None], (peers, *array.shape)), axis, 0, 0, tiled=True
    )


def of_everyone(array, axis):
    everything = from_everyone(array, axis)
    return jnp.max(everything, axis=0)


def split_up(array, dim, peers):
    shape = array.shape
    pieces = array.reshape(*shape[:dim], peers, shape[dim] // peers, *shape[dim + 1 :])
    return jnp.moveaxis(pieces, dim, 0)


def sum_at_owner(array, axis, dim):
    pieces = split_up(array, dim, lax.axis_size(axis))
    arrived = lax.all_to_all(pieces, axis, split_axis=0, concat_axis=0, tiled=True)
    return arrived.sum(axis=0)


def in_one_piece(arrays, axis, dim, along):
    widths = [math.prod(a.shape[along:]) for a in arrays]
    both = jnp.concatenate(
        [a.reshape(*a.shape[:along], w) for a, w in zip(arrays, widths)], axis=along
    )
    result = sum_at_owner(both, axis, dim)
    pieces = jnp.split(result, [sum(widths[:k]) for k in range(1, len(widths))], axis=along)
    return tuple(
        (b.reshape(*result.shape[:along], *a.shape[along:]) for a, b in zip(arrays, pieces))
    )


def laid_out(pieces, dim):
    pieces = jnp.moveaxis(pieces, 0, dim)
    shape = pieces.shape
    return pieces.reshape(*shape[:dim], shape[dim] * shape[dim + 1], *shape[dim + 2 :])


def gather_directly(array, axis, dim):
    pieces = from_everyone(array, axis)
    return laid_out(pieces, dim)


def ancestors(parent_row):
    tree_size = parent_row.shape[0]
    indices = jnp.arange(tree_size, dtype=jnp.int32)
    parent_link = (parent_row[:, None] == indices[None, :]).astype(jnp.float32)
    itself = (indices[:, None] == indices[None, :]).astype(jnp.float32)
    reached = jnp.maximum(parent_link, itself)
    for repeat in range(max(1, (tree_size - 1).bit_length())):
        reached = jnp.minimum(jnp.dot(reached, reached, precision=lax.Precision.HIGHEST), 1.0)
    return reached


def partial_scores(query_rows, keys, values, allowed, score_scale):
    scores = (
        jnp.einsum("kqd,pkd->kqp", query_rows, keys, preferred_element_type=jnp.float32)
        * score_scale
    )
    scores = jnp.where(allowed, scores, lowest)
    maxima = jnp.max(scores, axis=-1)
    weights = jnp.where(allowed, jnp.exp(scores - maxima[..., None]), 0.0)
    totals = jnp.sum(weights, axis=-1)
    weighted = jnp.einsum(
        "kqp,pkd->kqd", weights.astype(jnp.bfloat16), values, preferred_element_type=jnp.float32
    )
    return (maxima, totals, weighted)


def body(queries, new_keys, new_values, cache_keys, cache_values, parents, kv_lengths, out_weight):
    requests, tree_size, heads, head_size = queries.shape
    kv_heads = new_keys.shape[2]
    group_size = heads // kv_heads
    block_size = cache_keys.shape[1]
    score_scale = 1.0 / math.sqrt(head_size)
    tokens = requests * tree_size
    positions = lax.axis_index("seq") * block_size + jnp.arange(block_size, dtype=jnp.int32)

    def token_order(maxima, totals, weighted):
        maxima = (
            maxima.reshape(kv_heads, tree_size, group_size)
            .transpose(1, 0, 2)
            .reshape(tree_size, heads)
        )
        totals = (
            totals.reshape(kv_heads, tree_size, group_size)
            .transpose(1, 0, 2)
            .reshape(tree_size, heads)
        )
        weighted = weighted.reshape(kv_heads, tree_size, group_size, head_size).transpose(
            1, 0, 2, 3
        )
        return (maxima, totals, weighted.reshape(tree_size, heads, head_size))

    def one_request(request_items):
        query, tree_keys, tree_values, past_keys, past_values, parent_row, length = request_items
        query_rows = query.reshape(tree_size, kv_heads, group_size, head_size).transpose(1, 0, 2, 3)
        query_rows = query_rows.reshape(kv_heads, tree_size * group_size, head_size)
        cache_max, cache_tot, cache_acc = partial_scores(
            query_rows, past_keys, past_values, positions < length, score_scale
        )
        tree_allowed = jnp.repeat(ancestors(parent_row), group_size, axis=0) > 0.5
        tree_max, tree_tot, tree_acc = partial_scores(
            query_rows, tree_keys, tree_values, tree_allowed, score_scale
        )
        return (
            token_order(cache_max, cache_tot, cache_acc),
            token_order(tree_max, tree_tot, tree_acc),
        )

    cache_part, tree_part = lax.map(
        one_request, (queries, new_keys, new_values, cache_keys, cache_values, parents, kv_lengths)
    )
    cache_max = cache_part[0].reshape(tokens, heads)
    cache_tot = cache_part[1].reshape(tokens, heads)
    cache_acc = cache_part[2].reshape(tokens, heads, head_size)
    tree_max = tree_part[0].reshape(tokens, heads)
    tree_tot = tree_part[1].reshape(tokens, heads)
    tree_acc = tree_part[2].reshape(tokens, heads, head_size)
    overall = of_everyone(cache_max, "seq")
    overall = jnp.maximum(overall, tree_max)
    factor = jnp.exp(cache_max - overall)
    shared_acc, shared_tot = in_one_piece(
        (cache_acc * factor[..., None], cache_tot * factor), "seq", 0, 2
    )
    row_count = tokens // lax.axis_size("seq")
    first_row = lax.axis_index("seq") * row_count

    def take_rows(array):
        return lax.dynamic_slice_in_dim(array, first_row, row_count, 0)

    tree_factor = jnp.exp(take_rows(tree_max) - take_rows(overall))
    weighted = shared_acc + take_rows(tree_acc) * tree_factor[..., None]
    totals = shared_tot + take_rows(tree_tot) * tree_factor
    share = (
        (weighted / totals[..., None]).astype(jnp.bfloat16).reshape(row_count, heads * head_size)
    )
    attended = gather_directly(share, "seq", 0)
    mixed = sum_at_owner(
        jnp.dot(attended, out_weight, preferred_element_type=jnp.float32), "head", 0
    )
    return mixed.astype(jnp.bfloat16)


def solution(mesh):
    placed = (
        P(None, None, "head", None),
        P(None, None, "head", None),
        P(None, None, "head", None),
        P(None, "seq", "head", None),
        P(None, "seq", "head", None),
        P(),
        P(),
        P("head", "seq"),
    )
    return jax.shard_map(
        body, mesh=mesh, in_specs=placed, out_specs=P("head", "seq"), check_vma=False
    )
```

profile of v0, /device:TPU:1, one launch (start us, length us, event | category | flops | bytes accessed | tf_op | source)
XLA Modules:
  0.0 168.7 jit_solution(10875792629119249173)
XLA Ops:
  0.0 48.6 %while.21 = (s32[]{:T(128)}, f32[4,64,8]{2,1,0:T(8,128)S(1)}, f32[4,64,8]{2,1,0:T(8,128)S(1)}, f32[4,64,8,128]{3,2,1,0:T(8,128)S(1)}, f32[4,64,8]{2,1,0:T(8,128)...) while((s32[]{:T(128)}, f32[4,64,8]{2,1,0:T(8,128)S(1)}, ...), condition=%wide.region_5.6_spmd.clone, body=%wide.region_0.5_spmd.clone.sunk | while | flops 586434560 | bytes 15616949 | solution.py:125
  0.1 1.3 dynamic_slice.108
  1.3 0.6 add_compare_fusion.2
  1.9 2.0 %fusion.103 = (f32[512]{0:T(512)S(1)}, f32[512,2048]{1,0:T(8,128)S(1)}) fusion(pred[2048]{0:T(1024)(128)(4,1)S(1)} %add_compare_fusion.2, bf16[4,2048,1,128]{3,1,2,0:T(8,128)(2,1)} %get-tuple-element.322, s32[]{:T(128)} %get-tuple-element.297, bf16[4,64,8,128]{3,2,1,0:T(8,128)(2,1)} %get-tuple-element.321), kind=kOutput, calls=%fused_computation.3.clone.1 | convolution fusion | flops 271580672 | bytes 4854784 | tf_op jit(solution)/shard_map/while/body/eval_jaxpr/kqd,pkd->kqp/dot_general | solution.py:71
  3.9 2.0 %fusion.105 = f32[4,64,8,128]{3,2,1,0:T(8,128)S(1)} fusion(f32[4,64,8,128]{3,2,1,0:T(8,128)S(1)} %get-tuple-element.300, s32[]{:T(128)} %get-tuple-element.297, f32[512,2048]{1,0:T(8,128)S(1)} %get-tuple-element.271, f32[512]{0:T(512)S(1)} %get-tuple-element.272, pred[2048]{0:T(1024)(128)(4,1)S(1)} %add_compare_fusion.2, ...), kind=kOutput, calls=%fused_computation.10.clone.1 | convolution fusion | flops 273678336 | bytes 4985856 | tf_op jit(solution)/shard_map/while/body/eval_jaxpr/kqp,pkd->kqd/dot_general | solution.py:78
  5.9 1.1 fusion.104
  7.2 0.7 fusion.106
  7.9 0.2 convolution_minimum_fusion.11
  8.1 0.2 convolution_minimum_fusion.12
  8.3 0.2 convolution_minimum_fusion.13
  8.6 0.2 convolution_minimum_fusion.15
  8.8 0.2 fusion.107
  9.1 1.1 fusion.108
  10.4 1.6 fusion.110
  12.2 1.2 dynamic_slice.108
  13.5 0.6 add_compare_fusion.2
  14.1 2.0 %fusion.103 = (f32[512]{0:T(512)S(1)}, f32[512,2048]{1,0:T(8,128)S(1)}) fusion(pred[2048]{0:T(1024)(128)(4,1)S(1)} %add_compare_fusion.2, bf16[4,2048,1,128]{3,1,2,0:T(8,128)(2,1)} %get-tuple-element.322, s32[]{:T(128)} %get-tuple-element.297, bf16[4,64,8,128]{3,2,1,0:T(8,128)(2,1)} %get-tuple-element.321), kind=kOutput, calls=%fused_computation.3.clone.1 | convolution fusion | flops 271580672 | bytes 4854784 | tf_op jit(solution)/shard_map/while/body/eval_jaxpr/kqd,pkd->kqp/dot_general | solution.py:71
  16.0 2.0 %fusion.105 = f32[4,64,8,128]{3,2,1,0:T(8,128)S(1)} fusion(f32[4,64,8,128]{3,2,1,0:T(8,128)S(1)} %get-tuple-element.300, s32[]{:T(128)} %get-tuple-element.297, f32[512,2048]{1,0:T(8,128)S(1)} %get-tuple-element.271, f32[512]{0:T(512)S(1)} %get-tuple-element.272, pred[2048]{0:T(1024)(128)(4,1)S(1)} %add_compare_fusion.2, ...), kind=kOutput, calls=%fused_computation.10.clone.1 | convolution fusion | flops 273678336 | bytes 4985856 | tf_op jit(solution)/shard_map/while/body/eval_jaxpr/kqp,pkd->kqd/dot_general | solution.py:78
  18.0 1.1 fusion.104
  19.3 0.7 fusion.106
  20.0 0.2 convolution_minimum_fusion.11
  20.3 0.2 convolution_minimum_fusion.12
  20.4 0.2 convolution_minimum_fusion.13
  20.6 0.2 convolution_minimum_fusion.14
  20.8 0.2 convolution_minimum_fusion.15
  20.9 0.2 fusion.107
  21.3 1.1 fusion.108
  22.6 1.6 fusion.110
  24.4 1.2 dynamic_slice.108
  25.6 0.6 add_compare_fusion.2
  26.2 2.0 %fusion.103 = (f32[512]{0:T(512)S(1)}, f32[512,2048]{1,0:T(8,128)S(1)}) fusion(pred[2048]{0:T(1024)(128)(4,1)S(1)} %add_compare_fusion.2, bf16[4,2048,1,128]{3,1,2,0:T(8,128)(2,1)} %get-tuple-element.322, s32[]{:T(128)} %get-tuple-element.297, bf16[4,64,8,128]{3,2,1,0:T(8,128)(2,1)} %get-tuple-element.321), kind=kOutput, calls=%fused_computation.3.clone.1 | convolution fusion | flops 271580672 | bytes 4854784 | tf_op jit(solution)/shard_map/while/body/eval_jaxpr/kqd,pkd->kqp/dot_general | solution.py:71
  28.1 2.0 %fusion.105 = f32[4,64,8,128]{3,2,1,0:T(8,128)S(1)} fusion(f32[4,64,8,128]{3,2,1,0:T(8,128)S(1)} %get-tuple-element.300, s32[]{:T(128)} %get-tuple-element.297, f32[512,2048]{1,0:T(8,128)S(1)} %get-tuple-element.271, f32[512]{0:T(512)S(1)} %get-tuple-element.272, pred[2048]{0:T(1024)(128)(4,1)S(1)} %add_compare_fusion.2, ...), kind=kOutput, calls=%fused_computation.10.clone.1 | convolution fusion | flops 273678336 | bytes 4985856 | tf_op jit(solution)/shard_map/while/body/eval_jaxpr/kqp,pkd->kqd/dot_general | solution.py:78
  30.1 1.1 fusion.104
  31.4 0.7 fusion.106
  32.1 0.2 convolution_minimum_fusion.11
  32.9 0.2 convolution_minimum_fusion.15
  33.1 0.2 fusion.107
  33.4 1.1 fusion.108
  34.7 1.6 fusion.110
  36.5 1.2 dynamic_slice.108
  37.7 0.6 add_compare_fusion.2
  38.3 2.0 %fusion.103 = (f32[512]{0:T(512)S(1)}, f32[512,2048]{1,0:T(8,128)S(1)}) fusion(pred[2048]{0:T(1024)(128)(4,1)S(1)} %add_compare_fusion.2, bf16[4,2048,1,128]{3,1,2,0:T(8,128)(2,1)} %get-tuple-element.322, s32[]{:T(128)} %get-tuple-element.297, bf16[4,64,8,128]{3,2,1,0:T(8,128)(2,1)} %get-tuple-element.321), kind=kOutput, calls=%fused_computation.3.clone.1 | convolution fusion | flops 271580672 | bytes 4854784 | tf_op jit(solution)/shard_map/while/body/eval_jaxpr/kqd,pkd->kqp/dot_general | solution.py:71
  40.3 2.0 %fusion.105 = f32[4,64,8,128]{3,2,1,0:T(8,128)S(1)} fusion(f32[4,64,8,128]{3,2,1,0:T(8,128)S(1)} %get-tuple-element.300, s32[]{:T(128)} %get-tuple-element.297, f32[512,2048]{1,0:T(8,128)S(1)} %get-tuple-element.271, f32[512]{0:T(512)S(1)} %get-tuple-element.272, pred[2048]{0:T(1024)(128)(4,1)S(1)} %add_compare_fusion.2, ...), kind=kOutput, calls=%fused_computation.10.clone.1 | convolution fusion | flops 273678336 | bytes 4985856 | tf_op jit(solution)/shard_map/while/body/eval_jaxpr/kqp,pkd->kqd/dot_general | solution.py:78
  42.2 1.1 fusion.104
  43.5 0.7 fusion.106
  44.2 0.2 convolution_minimum_fusion.11
  44.5 0.2 convolution_minimum_fusion.12
  44.7 0.2 convolution_minimum_fusion.13
  45.2 0.2 fusion.107
  45.5 1.1 fusion.108
  46.8 1.6 fusion.110
  48.7 0.7 broadcast_in_dim.65
  49.4 11.1 %all-to-all-start = ((f32[32,256,8]{1,2,0:T(8,128)}), f32[32,256,8]{1,2,0:T(8,128)S(1)}, u32[]{:S(2)}, u32[]{:S(2)}) async-start(f32[32,256,8]{1,2,0:T(8,128)} %broadcast_in_dim.65), calls=%async_computation | async-start | bytes 524288 | tf_op jit(solution)/shard_map/all_to_all | solution.py:13
  61.3 10.8 %all-to-all-done = f32[32,256,8]{1,2,0:T(8,128)S(1)} async-done(((f32[32,256,8]{1,2,0:T(8,128)}), f32[32,256,8]{1,2,0:T(8,128)S(1)}, u32[]{:S(2)}, u32[]{:S(2)}) %all-to-all-start) | async-done | bytes 262176 | tf_op jit(solution)/shard_map/all_to_all | solution.py:13
  72.5 1.6 copy.83
  74.1 0.3 broadcast_multiply_fusion
  74.4 1.6 pad_maximum_fusion
  76.0 5.5 %all-to-all-start.1 = ((f32[32,8,8,129]{3,2,1,0:T(8,128)}), f32[32,8,8,129]{3,2,1,0:T(8,128)S(1)}, u32[]{:S(2)}, u32[]{:S(2)}) async-start(f32[32,8,8,129]{3,2,1,0:T(8,128)} %pad_maximum_fusion), calls=%async_computation.1 | async-start | bytes 4194304 | tf_op jit(solution)/shard_map/all_to_all | solution.py:31
  81.7 49.2 %all-to-all-done.1 = f32[32,8,8,129]{3,2,1,0:T(8,128)S(1)} async-done(((f32[32,8,8,129]{3,2,1,0:T(8,128)}), f32[32,8,8,129]{3,2,1,0:T(8,128)S(1)}, u32[]{:S(2)}, u32[]{:S(2)}) %all-to-all-start.1) | async-done | bytes 1056800 | tf_op jit(solution)/shard_map/all_to_all | solution.py:31
  131.4 0.8 fusion.50
  132.3 22.0 %all_to_all.20 = bf16[32,8,1024]{2,1,0:T(8,128)(2,1)S(1)} all-to-all(bf16[32,8,1024]{2,1,0:T(8,128)(2,1)S(1)} %broadcast_in_dim.67), channel_id=1, replica_groups=mesh['seq'=32,'head'=8] {'seq'}, dimensions={0} | all-to-all | bytes 1048576 | tf_op jit(solution)/shard_map/all_to_all | solution.py:13
  154.3 0.3 fusion.46
  154.6 13.5 %all_to_all.21 = f32[8,32,256]{2,1,0:T(8,128)S(1)} all-to-all(f32[8,32,256]{2,1,0:T(8,128)S(1)} %fusion.46), channel_id=1, replica_groups=mesh['seq'=32,'head'=8] {'head'}, dimensions={0} | all-to-all | bytes 524288 | tf_op jit(solution)/shard_map/all_to_all | solution.py:31
  168.1 0.6 reduce_sum.37
  (77 shorter events, 5.7 us)
Async XLA Ops:
  0.0 154.3 %copy-start = (bf16[1024,256]{1,0:T(8,128)(2,1)S(1)}, bf16[1024,256]{1,0:T(8,128)(2,1)}, u32[]{:S(2)}) copy-start(bf16[1024,256]{1,0:T(8,128)(2,1)} %param.17) | copy-start | bytes 1572868
  49.4 22.7 %all-to-all-start = ((f32[32,256,8]{1,2,0:T(8,128)}), f32[32,256,8]{1,2,0:T(8,128)S(1)}, u32[]{:S(2)}, u32[]{:S(2)}) async-start(f32[32,256,8]{1,2,0:T(8,128)} %broadcast_in_dim.65), calls=%async_computation | async-start | bytes 524288 | tf_op jit(solution)/shard_map/all_to_all | solution.py:13
  76.0 54.9 %all-to-all-start.1 = ((f32[32,8,8,129]{3,2,1,0:T(8,128)}), f32[32,8,8,129]{3,2,1,0:T(8,128)S(1)}, u32[]{:S(2)}, u32[]{:S(2)}) async-start(f32[32,8,8,129]{3,2,1,0:T(8,128)} %pad_maximum_fusion), calls=%async_computation.1 | async-start | bytes 4194304 | tf_op jit(solution)/shard_map/all_to_all | solution.py:31
where the time goes:
time: 171 us; the launch traced here: 169 us
  waiting for transfers between devices  60 us (35%)
  blocking collectives  35.5 us (21%)
  matrix products  31.1 us (18%)
  starting transfers between devices  16.6 us (10%)
  local copies, waits for them, and re-layouts  14.2 us (8%)
  other arithmetic  10.5 us (6%)
    all_to_all x1, waiting for transfers between devices, sum_at_owner(): lax.all_to_all(pieces, axis, split_axis=0, concat_axis=0, tiled=True)  49.2 us
    all_to_all x1, blocking collectives, from_everyone(): lax.all_to_all(jnp.broadcast_to(array[None], (peers, *array.shape)), axis...  22 us
    dot_general x8, matrix products, partial_scores(): jnp.einsum('kqp,pkd->kqd', weights.astype(jnp.bfloat16), values, preferre...  14.4 us
    all_to_all x1, blocking collectives, sum_at_owner(): lax.all_to_all(pieces, axis, split_axis=0, concat_axis=0, tiled=True)  13.5 us
    dot_general x8, matrix products, partial_scores(): jnp.einsum('kqd,pkd->kqp', query_rows, keys, preferred_element_type=jnp.f...  12.3 us
    all_to_all x1, starting transfers between devices, from_everyone(): lax.all_to_all(jnp.broadcast_to(array[None], (peers, *array.shape)), axis...  11.1 us
    all_to_all x1, waiting for transfers between devices, from_everyone(): lax.all_to_all(jnp.broadcast_to(array[None], (peers, *array.shape)), axis...  10.8 us
    all_to_all x1, starting transfers between devices, sum_at_owner(): lax.all_to_all(pieces, axis, split_axis=0, concat_axis=0, tiled=True)  5.5 us
  transfers between devices with their start and end apart: 2, of which 2 were waited for; matrix products, arithmetic and copies ran while one was open for 1% of the time, Pallas kernels for 0%

commit v1 on v0

v1 whole, which is shorter than its diff:
```python
import functools
import math

import jax
import jax.numpy as jnp
from jax import lax
from jax.experimental import pallas as pl
from jax.experimental.pallas import tpu as pltpu
from jax.sharding import PartitionSpec as P

lowest = -1e30
lanes = 128
dims_last = (((1,), (1,)), ((), ()))
dims_mid = (((1,), (0,)), ((), ()))


def iota(shape, dim):
    return lax.broadcasted_iota(jnp.int32, shape, dim)


def f32dot(a, b, dims=dims_mid):
    return lax.dot_general(a, b, dims, preferred_element_type=jnp.float32)


def regroup(count, heads):
    rows, cols = iota((count * heads, count * heads), 0), iota((count * heads, count * heads), 1)
    return (cols == (rows % count) * heads + rows // count).astype(jnp.bfloat16)


def put_stats(maxima, totals, count, heads):
    lane = iota((count, lanes), 1)
    stats = jnp.zeros((count, lanes), jnp.float32)
    high = totals.astype(jnp.bfloat16).astype(jnp.float32)
    low = totals - high
    for h in range(heads):
        part = slice(h * count, (h + 1) * count)
        stats = jnp.where(lane == h, maxima[part], stats)
        stats = jnp.where(lane == heads + h, high[part], stats)
        stats = jnp.where(lane == 2 * heads + h, low[part], stats)
    return stats


def cache_kernel(where, lengths, query, keys, values, out, scores, *, scale, chunk):
    count, heads, size = query.shape[1:]
    rows = count * heads
    block = keys.shape[1]
    valid = lengths[where[0] + pl.program_id(0)] - where[1]
    width = heads * size

    def work(masked):
        turned = f32dot(regroup(count, heads), query[0].reshape(rows, size)).astype(jnp.bfloat16)
        best = None
        for c in range(block // chunk):
            part = f32dot(turned, keys[0, c * chunk : (c + 1) * chunk], dims_last)
            if masked:
                part = jnp.where(iota((1, chunk), 1) + c * chunk < valid, part, lowest)
            scores[:, c * chunk : (c + 1) * chunk] = part
            for j in range(chunk // lanes):
                piece = part[:, j * lanes : (j + 1) * lanes]
                best = piece if best is None else jnp.maximum(best, piece)
        top = jnp.max(best, axis=1, keepdims=True) * scale
        top = top.astype(jnp.bfloat16).astype(jnp.float32)
        total = None
        for c in range(block // chunk):
            part = slice(c * chunk, (c + 1) * chunk)
            weights = jnp.exp2(scores[:, part] * scale - top).astype(jnp.bfloat16)
            wide = jnp.concatenate([values[0, part], jnp.ones((chunk, lanes), jnp.bfloat16)], axis=1)
            added = f32dot(weights, wide)
            total = added if total is None else total + added
        for h in range(heads):
            out[:, h * size : (h + 1) * size] = total[h * count : (h + 1) * count, :size].astype(out.dtype)
        stats = put_stats(jnp.broadcast_to(top, (rows, lanes)), total[:, size:], count, heads)
        out[:, width:] = stats.astype(out.dtype)

    @pl.when(valid >= block)
    def _():
        work(False)

    @pl.when((valid > 0) & (valid < block))
    def _():
        work(True)

    @pl.when(valid <= 0)
    def _():
        out[:, :width] = jnp.zeros((count, width), out.dtype)
        lane = iota((count, lanes), 1)
        out[:, width:] = jnp.where(lane < heads, lowest, 0.0).astype(out.dtype)


def cache_part(where, lengths, queries, keys, values, number, dtype, scale):
    _, count, heads, size = queries.shape
    block = keys.shape[1]
    width = heads * size + lanes
    return pl.pallas_call(
        functools.partial(cache_kernel, scale=scale, chunk=512),
        grid_spec=pltpu.PrefetchScalarGridSpec(
            num_scalar_prefetch=2,
            grid=(number,),
            in_specs=[
                pl.BlockSpec((1, count, heads, size), lambda i, w, n: (w[0] + i, 0, 0, 0)),
                pl.BlockSpec((1, block, size), lambda i, w, n: (w[0] + i, 0, 0)),
                pl.BlockSpec((1, block, size), lambda i, w, n: (w[0] + i, 0, 0)),
            ],
            out_specs=pl.BlockSpec((count, width), lambda i, w, n: (i, 0)),
            scratch_shapes=[pltpu.VMEM((count * heads, block), jnp.float32)],
        ),
        out_shape=jax.ShapeDtypeStruct((number * count, width), dtype),
        name="cache_part",
    )(where, lengths, queries, keys, values)


def join_kernel(mine, other, out, *, heads, size):
    count = mine.shape[0]
    width = heads * size
    a, b = mine[:, width:].astype(jnp.float32), other[:, width:].astype(jnp.float32)
    lane = iota((count, lanes), 1)
    top = jnp.maximum(a, b)
    fa, fb = jnp.exp2(a - top), jnp.exp2(b - top)
    fa = jnp.where(lane < heads, fa, 0.0)
    fb = jnp.where(lane < heads, fb, 0.0)
    high = a * pltpu.roll(fa, heads, 1) + b * pltpu.roll(fb, heads, 1)
    low = a * pltpu.roll(fa, 2 * heads, 1) + b * pltpu.roll(fb, 2 * heads, 1)
    total = high + pltpu.roll(low, lanes - heads, 1)
    high = total.astype(jnp.bfloat16).astype(jnp.float32)
    low = pltpu.roll(total - high, heads, 1)
    stats = jnp.where(lane < heads, top, jnp.where(lane < 2 * heads, high, low))
    out[:, width:] = stats.astype(out.dtype)
    for h in range(heads):
        part = slice(h * size, (h + 1) * size)
        sum_ = mine[:, part].astype(jnp.float32) * fa[:, h : h + 1]
        sum_ = sum_ + other[:, part].astype(jnp.float32) * fb[:, h : h + 1]
        out[:, part] = sum_.astype(out.dtype)


def join(mine, other, heads, size):
    return pl.pallas_call(
        functools.partial(join_kernel, heads=heads, size=size),
        out_shape=jax.ShapeDtypeStruct(other.shape, jnp.bfloat16),
        name="join",
    )(mine, other)


def tree_kernel(where, query, keys, values, parents, out, *, scale):
    count, heads, size = query.shape[1:]
    tree = keys.shape[1]
    width = heads * size
    parent_row = parents[pl.ds(where[0], 1), :]
    j, i = iota((tree, tree), 0), iota((tree, tree), 1)
    reached = ((parent_row == j) | (i == j)).astype(jnp.bfloat16)
    for repeat in range(max(1, (tree - 1).bit_length())):
        reached = jnp.minimum(f32dot(reached, reached), 1.0).astype(jnp.bfloat16)
    own = iota((count, tree), 1) == iota((count, tree), 0) + where[1] * count
    allowed = f32dot(own.astype(jnp.bfloat16), reached, dims_last) > 0.5
    rows = count * heads
    turned = f32dot(regroup(count, heads), query[0].reshape(rows, size)).astype(jnp.bfloat16)
    s = f32dot(turned, keys[0], dims_last).reshape(heads, count, tree)
    s = jnp.where(allowed[None], s * scale, lowest).reshape(rows, tree)
    top = jnp.max(s, axis=1, keepdims=True)
    weights = jnp.exp2(s - top).astype(jnp.bfloat16)
    wide = jnp.concatenate([values[0], jnp.ones((tree, lanes), jnp.bfloat16)], axis=1)
    total = f32dot(weights, wide)
    for h in range(heads):
        out[:, h * size : (h + 1) * size] = total[h * count : (h + 1) * count, :size]
    out[:, width:] = put_stats(jnp.broadcast_to(top, (rows, lanes)), total[:, size:], count, heads)


def tree_part(where, queries, keys, values, parents, count, scale):
    _, tree, heads, size = queries.shape
    width = heads * size + lanes
    return pl.pallas_call(
        functools.partial(tree_kernel, scale=scale),
        grid_spec=pltpu.PrefetchScalarGridSpec(
            num_scalar_prefetch=1,
            grid=(1,),
            in_specs=[
                pl.BlockSpec((1, count, heads, size), lambda i, w: (w[0], w[1], 0, 0)),
                pl.BlockSpec((1, tree, size), lambda i, w: (w[0], 0, 0)),
                pl.BlockSpec((1, tree, size), lambda i, w: (w[0], 0, 0)),
                pl.BlockSpec(parents.shape, lambda i, w: (0, 0)),
            ],
            out_specs=pl.BlockSpec((count, width), lambda i, w: (0, 0)),
        ),
        out_shape=jax.ShapeDtypeStruct((count, width), jnp.float32),
        name="tree_part",
    )(where, queries, keys, values, parents)


def finish_kernel(parts, own, out, *, heads, size):
    peers, count, _ = parts.shape
    width = heads * size
    lane = iota((count, lanes), 1)
    stats = [parts[p, :, width:].astype(jnp.float32) for p in range(peers)] + [own[:, width:]]
    top = stats[0]
    for s in stats[1:]:
        top = jnp.maximum(top, s)
    factors = [jnp.where(lane < heads, jnp.exp2(s - top), 0.0) for s in stats]
    high, low = jnp.zeros_like(top), jnp.zeros_like(top)
    for s, f in zip(stats, factors):
        high = high + s * pltpu.roll(f, heads, 1)
        low = low + s * pltpu.roll(f, 2 * heads, 1)
    total = pltpu.roll(high, lanes - heads, 1) + pltpu.roll(low, lanes - 2 * heads, 1)
    inverse = 1.0 / jnp.where(lane < heads, total, 1.0)
    for h in range(heads):
        part = slice(h * size, (h + 1) * size)
        merged = own[:, part] * factors[peers][:, h : h + 1]
        for p in range(peers):
            merged = merged + parts[p, :, part].astype(jnp.float32) * factors[p][:, h : h + 1]
        out[:, part] = (merged * inverse[:, h : h + 1]).astype(out.dtype)


def finish(parts, own, heads, size):
    return pl.pallas_call(
        functools.partial(finish_kernel, heads=heads, size=size),
        out_shape=jax.ShapeDtypeStruct((parts.shape[1], heads * size), jnp.bfloat16),
        name="finish",
    )(parts, own)


def project_kernel(which, mine, other, weight, out):
    count = mine.shape[0]
    first = pl.multiple_of(which[0] * count, count)
    second = pl.multiple_of((1 - which[0]) * count, count)
    out[pl.ds(first, count), :] = f32dot(mine[...], weight[...]).astype(out.dtype)
    out[pl.ds(second, count), :] = f32dot(other[...], weight[...]).astype(out.dtype)


def project(which, mine, other, weight):
    whole = lambda a: pl.BlockSpec(a.shape, lambda i, w: (0, 0))
    shape = (2 * mine.shape[0], weight.shape[1])
    return pl.pallas_call(
        project_kernel,
        grid_spec=pltpu.PrefetchScalarGridSpec(
            num_scalar_prefetch=1,
            grid=(1,),
            in_specs=[whole(mine), whole(other), whole(weight)],
            out_specs=pl.BlockSpec(shape, lambda i, w: (0, 0)),
        ),
        out_shape=jax.ShapeDtypeStruct(shape, jnp.bfloat16),
        name="project",
    )(which, mine, other, weight)


def body(queries, new_keys, new_values, cache_keys, cache_values, parents, kv_lengths, out_weight):
    requests, tree, heads, size = queries.shape
    peers = lax.axis_size("seq")
    head_peers = lax.axis_size("head")
    tokens = requests * tree
    block = cache_keys.shape[1]
    keys = cache_keys.reshape(requests, block, size)
    values = cache_values.reshape(requests, block, size)
    draft_keys = new_keys.reshape(requests, tree, size)
    draft_values = new_values.reshape(requests, tree, size)
    scale = math.log2(math.e) / math.sqrt(size)
    place = lax.axis_index("seq").astype(jnp.int32)
    core, chip = place % 2, place // 2
    half = requests // 2
    chips = peers // 2
    count = tokens // peers
    sibling = [(i, i ^ 1) for i in range(peers)]
    same_core = [[2 * i + c for i in range(chips)] for c in range(2)]

    def at(base):
        return jnp.stack([base, place * block]).astype(jnp.int32)

    sent = cache_part(at((1 - core) * half), kv_lengths, queries, keys, values, half, jnp.bfloat16, scale)
    arrived = lax.ppermute(sent, "seq", sibling)
    kept = cache_part(at(core * half), kv_lengths, queries, keys, values, half, jnp.float32, scale)
    pair = join(kept, arrived, heads, size)
    parts = lax.all_to_all(
        pair.reshape(chips, count, -1), "seq", 0, 0, tiled=True, axis_index_groups=same_core
    )
    first = core * (tokens // 2) + chip * count
    where = jnp.stack([first // tree, (first % tree) // count]).astype(jnp.int32)
    own = tree_part(where, queries, draft_keys, draft_values, parents, count, scale)
    share = finish(parts, own, heads, size)
    mine = lax.all_to_all(
        jnp.broadcast_to(share[None], (chips, *share.shape)),
        "seq", 0, 0, tiled=True, axis_index_groups=same_core,
    ).reshape(tokens // 2, heads * size)
    other = lax.ppermute(mine, "seq", sibling)
    partial = project(core[None], mine, other, out_weight)
    pieces = lax.all_to_all(
        partial.reshape(head_peers, tokens // head_peers, -1), "head", 0, 0, tiled=True
    )
    return pieces.astype(jnp.float32).sum(axis=0).astype(jnp.bfloat16)


def solution(mesh):
    placed = (
        P(None, None, "head", None),
        P(None, None, "head", None),
        P(None, None, "head", None),
        P(None, "seq", "head", None),
        P(None, "seq", "head", None),
        P(),
        P(),
        P("head", "seq"),
    )
    return jax.shard_map(
        body, mesh=mesh, in_specs=placed, out_specs=P("head", "seq"), check_vma=False
    )
```

time: 171 us -> 76 us (0.44)
  waiting for transfers between devices: 60 us -> 7.03 us
  matrix products: 31.1 us -> 0 us
  Pallas kernels: 0 us -> 22.8 us
  local copies, waits for them, and re-layouts: 14.2 us -> 2.86 us
  other arithmetic: 10.5 us -> 2.33 us
  blocking collectives: 35.5 us -> 27.4 us
  starting transfers between devices: 16.6 us -> 12.4 us
    all_to_all x2 -> x1, waiting for transfers between devices: 60 us -> 5.87 us  [body(): lax.all_to_all(pair.reshape(chips, count, -1), 'seq', 0, 0, tiled=True, a...]
    dot_general x41 -> x0, matrix products: 31.1 us -> none  [the longest x8 14.4 us: partial_scores(): jnp.einsum('kqp,pkd->kqd', weights.astype(jnp.bfloat16), values, preferre...]
    pallas_call x0 -> x6, Pallas kernels: none -> 22.8 us  [the longest x2 13.3 us: cache_part(): pl.pallas_call(functools.partial(cache_kernel, scale=scale, chunk=512), g...]
    all_to_all x2 -> x1, starting transfers between devices: 16.6 us -> 4.35 us  [body(): lax.all_to_all(pair.reshape(chips, count, -1), 'seq', 0, 0, tiled=True, a...]
    all_to_all x2, blocking collectives: 35.5 us -> 27.4 us  [the longest x1 13.8 us: body(): lax.all_to_all(jnp.broadcast_to(share[None], (chips, *share.shape)), 'seq...]
    ppermute x0 -> x2, starting transfers between devices: none -> 8.05 us  [the longest x1 5.44 us: body(): arrived = lax.ppermute(sent, 'seq', sibling)]
    dynamic_slice x5 -> x0, local copies, waits for them, and re-layouts: 5 us -> none  [the longest x4 4.99 us: body(): lax.map(one_request, (queries, new_keys, new_values, cache_keys, cache_va...]
    reduce_sum x6 -> x1, other arithmetic: 5.14 us -> 0.63 us  [body(): return pieces.astype(jnp.float32).sum(axis=0).astype(jnp.bfloat16)]
  transfers between devices with their start and end apart: 2 -> 3, of which waited for: 2 -> 2; matrix products, arithmetic and copies ran while one was open for 1% -> 2% of each run, Pallas kernels for 0% -> 15%
where the time goes in v1:
time: 76 us; the launch traced here: 74.9 us
  blocking collectives  27.4 us (36%)
  Pallas kernels  22.8 us (30%)
  starting transfers between devices  12.4 us (16%)
  waiting for transfers between devices  7.03 us (9%)
  local copies, waits for them, and re-layouts  2.86 us (4%)
  other arithmetic  2.33 us (3%)
    all_to_all x1, blocking collectives, body(): lax.all_to_all(jnp.broadcast_to(share[None], (chips, *share.shape)), 'seq...  13.8 us
    all_to_all x1, blocking collectives, body(): lax.all_to_all(partial.reshape(head_peers, tokens // head_peers, -1), 'he...  13.6 us
    pallas_call x2, Pallas kernels, cache_part(): pl.pallas_call(functools.partial(cache_kernel, scale=scale, chunk=512), g...  13.3 us
    all_to_all x1, waiting for transfers between devices, body(): lax.all_to_all(pair.reshape(chips, count, -1), 'seq', 0, 0, tiled=True, a...  5.87 us
    ppermute x1, starting transfers between devices, body(): arrived = lax.ppermute(sent, 'seq', sibling)  5.44 us
    all_to_all x1, starting transfers between devices, body(): lax.all_to_all(pair.reshape(chips, count, -1), 'seq', 0, 0, tiled=True, a...  4.35 us
    pallas_call x1, Pallas kernels, tree_part(): pl.pallas_call(functools.partial(tree_kernel, scale=scale), grid_spec=plt...  3.13 us
    ppermute x1, starting transfers between devices, body(): other = lax.ppermute(mine, 'seq', sibling)  2.62 us
  transfers between devices with their start and end apart: 3, of which 2 were waited for; matrix products, arithmetic and copies ran while one was open for 2% of the time, Pallas kernels for 15%

profile of v1, /device:TPU:1, one launch (start us, length us, event | category | flops | bytes accessed | tf_op | source)
XLA Modules:
  0.0 74.9 jit_solution(8497070209862520734)
XLA Ops:
  0.0 0.6 pad_add_fusion.1.where
  0.6 5.5 %cache_part.3 = bf16[128,1152]{1,0:T(8,128)(2,1)} custom-call(s32[2]{0:T(128)} %pad_add_fusion.1.where, s32[4]{0:T(128)} %lengths.3, bf16[4,64,8,128]{3,2,1,0:T(8,128)(2,1)} %query.5, bf16[4,2048,128]{2,1,0:T(8,128)(2,1)} %bitcast.13, bf16[4,2048,128]{2,1,0:T(8,128)(2,1)} %bitcast.15), custom_call_target="tpu_custom_call" | custom-call | tf_op jit(solution)/shard_map/cache_part/pallas_call | solution.py:94
  6.1 5.4 %collective-permute-start = (bf16[128,1152]{1,0:T(8,128)(2,1)}, bf16[128,1152]{1,0:T(8,128)(2,1)S(1)}, u32[]{:S(2)}, u32[]{:S(2)}) collective-permute-start(bf16[128,1152]{1,0:T(8,128)(2,1)} %cache_part.3), channel_id=1, source_target_pairs={{0,8},{8,0},{16,24},{24,16},{32,40},{40,32},{48,56},{56,48},{64,72... | collective-permute-start | bytes 884744 | tf_op jit(solution)/shard_map/ppermute | solution.py:266
  11.5 0.6 pad_add_fusion.where
  12.1 7.8 %cache_part.2.mine = f32[128,1152]{1,0:T(8,128)} custom-call(s32[2]{0:T(128)} %pad_add_fusion.where, s32[4]{0:T(128)} %lengths.3, bf16[4,64,8,128]{3,2,1,0:T(8,128)(2,1)} %query.5, bf16[4,2048,128]{2,1,0:T(8,128)(2,1)} %bitcast.14, bf16[4,2048,128]{2,1,0:T(8,128)(2,1)} %bitcast.16), custom_call_target="tpu_custom_call" | custom-call | tf_op jit(solution)/shard_map/cache_part/pallas_call | solution.py:94
  19.8 0.0 collective-permute-done.other
  19.8 0.0 copy-start.2
  19.8 0.7 copy-done.2
  20.6 2.4 %join.1 = bf16[128,1152]{1,0:T(8,128)(2,1)} custom-call(f32[128,1152]{1,0:T(8,128)} %cache_part.2.mine, bf16[128,1152]{1,0:T(8,128)(2,1)} %copy-done.2), custom_call_target="tpu_custom_call" | custom-call | tf_op jit(solution)/shard_map/join/pallas_call | solution.py:136
  22.9 4.3 %all-to-all-start = ((bf16[16,8,1152]{2,1,0:T(8,128)(2,1)}), bf16[16,8,1152]{2,1,0:T(8,128)(2,1)S(1)}, u32[]{:S(2)}, u32[]{:S(2)}) async-start(bf16[16,8,1152]{2,1,0:T(8,128)(2,1)} %bitcast.17), calls=%async_computation | async-start | bytes 589824 | tf_op jit(solution)/shard_map/all_to_all | solution.py:269
  27.3 0.6 pad_add_fusion.2.where
  27.9 3.1 %tree_part.1.own = f32[8,1152]{1,0:T(8,128)} custom-call(s32[2]{0:T(128)} %pad_add_fusion.2.where, bf16[4,64,8,128]{3,2,1,0:T(8,128)(2,1)} %query.5, bf16[4,64,128]{2,1,0:T(8,128)(2,1)} %bitcast.21, bf16[4,64,128]{2,1,0:T(8,128)(2,1)} %bitcast.22, s32[4,64]{1,0:T(4,128)} %parents.1), custom_call_target="tpu_custom_call" | custom-call | tf_op jit(solution)/shard_map/tree_part/pallas_call | solution.py:170
  31.1 5.9 %all-to-all-done.parts = bf16[16,8,1152]{2,1,0:T(8,128)(2,1)S(1)} async-done(((bf16[16,8,1152]{2,1,0:T(8,128)(2,1)}), bf16[16,8,1152]{2,1,0:T(8,128)(2,1)S(1)}, u32[]{:S(2)}, u32[]{:S(2)}) %all-to-all-start) | async-done | bytes 294944 | tf_op jit(solution)/shard_map/all_to_all | solution.py:269
  36.9 0.0 copy-start
  36.9 0.7 copy-done
  37.6 1.9 %finish.1 = bf16[8,1024]{1,0:T(8,128)(2,1)} custom-call(bf16[16,8,1152]{2,1,0:T(8,128)(2,1)} %copy-done, f32[8,1152]{1,0:T(8,128)} %tree_part.1.own), custom_call_target="tpu_custom_call" | custom-call | tf_op jit(solution)/shard_map/finish/pallas_call | solution.py:212
  39.5 0.7 broadcast_in_dim.10
  40.3 13.8 %all_to_all.15 = bf16[16,8,1024]{2,1,0:T(8,128)(2,1)S(1)} all-to-all(bf16[16,8,1024]{2,1,0:T(8,128)(2,1)S(1)} %broadcast_in_dim.10), channel_id=1, replica_groups={{0,16,32,48,64,80,96,112,128,144,160,176,192,208,224,240},{8,24,40,56,7..., dimensions={0} | all-to-all | bytes 524288 | tf_op jit(solution)/shard_map/all_to_all | solution.py:276
  54.1 0.0 copy-start.1
  54.1 2.6 %collective-permute-start.1 = (bf16[128,1024]{1,0:T(8,128)(2,1)S(1)}, bf16[128,1024]{1,0:T(8,128)(2,1)S(1)}, u32[]{:S(2)}, u32[]{:S(2)}) collective-permute-start(bf16[128,1024]{1,0:T(8,128)(2,1)S(1)} %bitcast.18), channel_id=1, source_target_pairs={{0,8},{8,0},{16,24},{24,16},{32,40},{40,32},{48,56},{56,48},{64,72... | collective-permute-start | bytes 786440 | tf_op jit(solution)/shard_map/ppermute | solution.py:280
  56.7 1.2 %collective-permute-done.1.other = bf16[128,1024]{1,0:T(8,128)(2,1)S(1)} collective-permute-done((bf16[128,1024]{1,0:T(8,128)(2,1)S(1)}, bf16[128,1024]{1,0:T(8,128)(2,1)S(1)}, u32[]{:S(2)}, u32[]{:S(2)}) %collective-permute-start.1) | collective-permute-done | bytes 262176 | tf_op jit(solution)/shard_map/ppermute | solution.py:280
  57.8 0.0 copy-start.3
  57.8 0.0 copy-done.1
  57.9 0.7 copy-done.3
  58.5 2.2 %project.1 = bf16[256,256]{1,0:T(8,128)(2,1)} custom-call(s32[1]{0:T(128)} %bitcast.which, bf16[128,1024]{1,0:T(8,128)(2,1)} %bitcast.19, bf16[128,1024]{1,0:T(8,128)(2,1)} %copy-done.3, bf16[1024,256]{1,0:T(8,128)(2,1)} %weight.1), custom_call_target="tpu_custom_call" | custom-call | tf_op jit(solution)/shard_map/project/pallas_call | solution.py:230
  60.7 13.6 %all_to_all.16 = bf16[8,32,256]{2,1,0:T(8,128)(2,1)S(1)} all-to-all(bf16[8,32,256]{2,1,0:T(8,128)(2,1)} %bitcast.20), channel_id=1, replica_groups=mesh['seq'=32,'head'=8] {'head'}, dimensions={0} | all-to-all | bytes 262144 | tf_op jit(solution)/shard_map/all_to_all | solution.py:282
  74.3 0.6 reduce_sum.12
Async XLA Ops:
  6.1 13.8 %collective-permute-start = (bf16[128,1152]{1,0:T(8,128)(2,1)}, bf16[128,1152]{1,0:T(8,128)(2,1)S(1)}, u32[]{:S(2)}, u32[]{:S(2)}) collective-permute-start(bf16[128,1152]{1,0:T(8,128)(2,1)} %cache_part.3), channel_id=1, source_target_pairs={{0,8},{8,0},{16,24},{24,16},{32,40},{40,32},{48,56},{56,48},{64,72... | collective-permute-start | bytes 884744 | tf_op jit(solution)/shard_map/ppermute | solution.py:266
  19.8 0.7 copy-start.2
  22.9 14.0 %all-to-all-start = ((bf16[16,8,1152]{2,1,0:T(8,128)(2,1)}), bf16[16,8,1152]{2,1,0:T(8,128)(2,1)S(1)}, u32[]{:S(2)}, u32[]{:S(2)}) async-start(bf16[16,8,1152]{2,1,0:T(8,128)(2,1)} %bitcast.17), calls=%async_computation | async-start | bytes 589824 | tf_op jit(solution)/shard_map/all_to_all | solution.py:269
  36.9 0.7 copy-start
  54.1 3.8 %copy-start.1 = (bf16[16,8,1024]{2,1,0:T(8,128)(2,1)}, bf16[16,8,1024]{2,1,0:T(8,128)(2,1)S(1)}, u32[]{:S(2)}) copy-start(bf16[16,8,1024]{2,1,0:T(8,128)(2,1)S(1)} %all_to_all.15) | copy-start | bytes 786436
  54.1 3.8 %collective-permute-start.1 = (bf16[128,1024]{1,0:T(8,128)(2,1)S(1)}, bf16[128,1024]{1,0:T(8,128)(2,1)S(1)}, u32[]{:S(2)}, u32[]{:S(2)}) collective-permute-start(bf16[128,1024]{1,0:T(8,128)(2,1)S(1)} %bitcast.18), channel_id=1, source_target_pairs={{0,8},{8,0},{16,24},{24,16},{32,40},{40,32},{48,56},{56,48},{64,72... | collective-permute-start | bytes 786440 | tf_op jit(solution)/shard_map/ppermute | solution.py:280
  57.8 0.7 copy-start.3

commit v2 on v1

v2 whole, which is shorter than its diff:
```python
import functools
import math

import jax
import jax.numpy as jnp
from jax import lax
from jax.experimental import pallas as pl
from jax.experimental.pallas import tpu as pltpu
from jax.sharding import PartitionSpec as P

lowest = -1e30
lanes = 128
dims_last = (((1,), (1,)), ((), ()))
dims_mid = (((1,), (0,)), ((), ()))
on_chip = pltpu.MemorySpace.VMEM


def iota(shape, dim):
    return lax.broadcasted_iota(jnp.int32, shape, dim)


def f32dot(a, b, dims=dims_mid):
    return lax.dot_general(a, b, dims, preferred_element_type=jnp.float32)


def here(array):
    return pltpu.with_memory_space_constraint(array, on_chip)


def away(array):
    return pltpu.with_memory_space_constraint(array, pltpu.MemorySpace.HBM)


def regroup(count, heads, total, first=0):
    row, col = iota((count, heads * total), 0), iota((count, heads * total), 1)
    start = (row + first) * heads
    return jnp.concatenate([(col == start + h).astype(jnp.bfloat16) for h in range(heads)], axis=0)


def put_stats(maxima, totals, count, heads):
    lane = iota((count, lanes), 1)
    stats = jnp.zeros((count, lanes), jnp.float32)
    high = totals.astype(jnp.bfloat16).astype(jnp.float32)
    low = totals - high
    for h in range(heads):
        part = slice(h * count, (h + 1) * count)
        stats = jnp.where(lane == h, maxima[part], stats)
        stats = jnp.where(lane == heads + h, high[part], stats)
        stats = jnp.where(lane == 2 * heads + h, low[part], stats)
    return stats


def attend(turned, keys, values, valid, out, scores, count, heads, scale, chunk, ready=None):
    rows, size = turned.shape
    block = keys.shape[0]
    width = heads * size
    halves = 2
    part_rows = rows // halves
    best = [None] * halves
    for c in range(block // chunk):
        where = slice(c * chunk, (c + 1) * chunk)
        allowed = iota((1, chunk), 1) + c * chunk < valid
        for g in range(halves):
            mine = slice(g * part_rows, (g + 1) * part_rows)
            part = f32dot(turned[mine], keys[where], dims_last)
            part = jnp.where(allowed, part, lowest)
            scores[mine, where] = part
            for j in range(chunk // lanes):
                piece = part[:, j * lanes : (j + 1) * lanes]
                best[g] = piece if best[g] is None else jnp.maximum(best[g], piece)
    tops = []
    for g in range(halves):
        top = jnp.max(best[g], axis=1, keepdims=True) * scale
        tops.append(top.astype(jnp.bfloat16).astype(jnp.float32))
    if ready is not None:
        ready()
    sums = [None] * halves
    for c in range(block // chunk):
        where = slice(c * chunk, (c + 1) * chunk)
        wide = jnp.concatenate([values[where], jnp.ones((chunk, lanes), jnp.bfloat16)], axis=1)
        for g in range(halves):
            mine = slice(g * part_rows, (g + 1) * part_rows)
            weights = jnp.exp2(scores[mine, where] * scale - tops[g]).astype(jnp.bfloat16)
            added = f32dot(weights, wide)
            sums[g] = added if sums[g] is None else sums[g] + added
    some = valid > 0
    total = jnp.concatenate([jnp.where(some, s, 0.0) for s in sums], axis=0)
    top = jnp.concatenate([jnp.where(some, jnp.broadcast_to(t, (part_rows, lanes)), lowest) for t in tops], axis=0)
    for h in range(heads):
        out[:, h * size : (h + 1) * size] = total[h * count : (h + 1) * count, :size].astype(out.dtype)
    out[:, width:] = put_stats(top, total[:, size:], count, heads).astype(out.dtype)


def draft(turned, keys, values, parent_row, first, out, heads, scale):
    rows, size = turned.shape
    count, tree, width = rows // heads, keys.shape[0], heads * size
    j, i = iota((tree, tree), 0), iota((tree, tree), 1)
    reached = ((parent_row == j) | (i == j)).astype(jnp.bfloat16)
    for repeat in range(max(1, (tree - 1).bit_length())):
        reached = jnp.minimum(f32dot(reached, reached), 1.0).astype(jnp.bfloat16)
    own = iota((count, tree), 1) == iota((count, tree), 0) + first
    allowed = f32dot(own.astype(jnp.bfloat16), reached, dims_last) > 0.5
    s = f32dot(turned, keys, dims_last).reshape(heads, count, tree)
    s = jnp.where(allowed[None], s * scale, lowest).reshape(rows, tree)
    top = jnp.max(s, axis=1, keepdims=True)
    weights = jnp.exp2(s - top).astype(jnp.bfloat16)
    wide = jnp.concatenate([values, jnp.ones((tree, lanes), jnp.bfloat16)], axis=1)
    total = f32dot(weights, wide)
    for h in range(heads):
        out[:, h * size : (h + 1) * size] = total[h * count : (h + 1) * count, :size]
    out[:, width:] = put_stats(jnp.broadcast_to(top, (rows, lanes)), total[:, size:], count, heads)


def send_kernel(
    lengths, parents, queries, draft_keys, draft_values, keys, values,
    sent, own, turned, kept_keys, kept_values,
    query, left_keys, left_values, left_turned, tree_keys, tree_values, scores, sems,
    *, scale, chunk, peers,
):
    requests, tree, heads, size = queries.shape
    block = keys.shape[1]
    half = requests // 2
    count = requests * tree // peers
    place = lax.axis_index("seq")
    core, chip = lax.rem(place, 2), lax.div(place, 2)
    mine, left = core * half, (1 - core) * half
    token = chip * count
    request, first = mine + lax.div(token, tree), lax.rem(token, tree)

    copies = [
        pltpu.make_async_copy(queries, query, sems.at[0]),
        pltpu.make_async_copy(draft_keys.at[request], tree_keys, sems.at[1]),
        pltpu.make_async_copy(draft_values.at[request], tree_values, sems.at[2]),
    ]
    for r in range(half):
        copies.append(pltpu.make_async_copy(keys.at[left + r], left_keys.at[r], sems.at[3 + 2 * r]))
        copies.append(pltpu.make_async_copy(values.at[left + r], left_values.at[r], sems.at[4 + 2 * r]))
    late = 3 + 2 * half
    copies.append(pltpu.make_async_copy(keys.at[pl.ds(mine, half)], kept_keys, sems.at[late]))
    copies.append(pltpu.make_async_copy(values.at[pl.ds(mine, half)], kept_values, sems.at[late + 1]))
    for copy in copies:
        copy.start()

    spin = regroup(tree, heads, tree)
    pick = regroup(count, heads, tree, first)
    copies[0].wait()
    for r in range(half):
        left_turned[r] = f32dot(spin, query[left + r].reshape(tree * heads, size)).astype(jnp.bfloat16)
        turned[r] = f32dot(spin, query[mine + r].reshape(tree * heads, size)).astype(jnp.bfloat16)
    picked = f32dot(pick, query[request].reshape(tree * heads, size)).astype(jnp.bfloat16)
    copies[1].wait()
    copies[2].wait()
    draft(picked, tree_keys[...], tree_values[...], parents[pl.ds(request, 1), :], first, own, heads, scale)
    for r in range(half):
        copies[3 + 2 * r].wait()
        attend(
            left_turned.at[r], left_keys.at[r], left_values.at[r], lengths[left + r] - place * block,
            sent.at[pl.ds(r * tree, tree)], scores, tree, heads, scale, chunk, copies[4 + 2 * r].wait,
        )
    copies[late].wait()
    copies[late + 1].wait()


def keep_kernel(lengths, turned, keys, values, out, scores, *, scale, chunk, tree):
    half, rows, size = turned.shape
    block = keys.shape[1]
    place = lax.axis_index("seq")
    mine = lax.rem(place, 2) * half
    for r in range(half):
        attend(
            turned.at[r], keys.at[r], values.at[r], lengths[mine + r] - place * block,
            out.at[pl.ds(r * tree, tree)], scores, tree, rows // tree, scale, chunk,
        )


def cache_parts(lengths, parents, queries, draft_keys, draft_values, keys, values, peers, scale, chunk=256):
    requests, tree, heads, size = queries.shape
    block = keys.shape[1]
    half = requests // 2
    rows, width = tree * heads, heads * size + lanes
    count = requests * tree // peers
    smem, vmem, far = (pl.BlockSpec(memory_space=m) for m in (pltpu.SMEM, pltpu.VMEM, pltpu.HBM))
    scores = pltpu.VMEM((rows, block), jnp.float32)
    bf16 = jnp.bfloat16
    limit = pltpu.CompilerParams(vmem_limit_bytes=24 << 20)
    sent, own, turned, kept_keys, kept_values = pl.pallas_call(
        functools.partial(send_kernel, scale=scale, chunk=chunk, peers=peers),
        in_specs=[smem, vmem, far, far, far, far, far],
        out_specs=[vmem] * 5,
        out_shape=[
            pltpu.VMEM((half * tree, width), bf16),
            pltpu.VMEM((count, width), jnp.float32),
            pltpu.VMEM((half, rows, size), bf16),
            pltpu.VMEM((half, block, size), bf16),
            pltpu.VMEM((half, block, size), bf16),
        ],
        scratch_shapes=[
            pltpu.VMEM((requests, tree, heads, size), bf16),
            pltpu.VMEM((half, block, size), bf16),
            pltpu.VMEM((half, block, size), bf16),
            pltpu.VMEM((half, rows, size), bf16),
            pltpu.VMEM((tree, size), bf16),
            pltpu.VMEM((tree, size), bf16),
            scores,
            pltpu.SemaphoreType.DMA((5 + 2 * half,)),
        ],
        compiler_params=limit,
        name="send_part",
    )(lengths, parents, *(away(a) for a in (queries, draft_keys, draft_values, keys, values)))
    arrived = lax.ppermute(sent, "seq", [(i, i ^ 1) for i in range(peers)])
    kept = pl.pallas_call(
        functools.partial(keep_kernel, scale=scale, chunk=chunk, tree=tree),
        in_specs=[smem, vmem, vmem, vmem],
        out_specs=vmem,
        out_shape=pltpu.VMEM((half * tree, width), jnp.float32),
        scratch_shapes=[scores],
        compiler_params=limit,
        name="keep_part",
    )(lengths, here(turned), here(kept_keys), here(kept_values))
    return kept, arrived, own


def join_kernel(mine, other, out, *, heads, size):
    count = mine.shape[0]
    width = heads * size
    a, b = mine[:, width:].astype(jnp.float32), other[:, width:].astype(jnp.float32)
    lane = iota((count, lanes), 1)
    top = jnp.maximum(a, b)
    fa = jnp.where(lane < heads, jnp.exp2(a - top), 0.0)
    fb = jnp.where(lane < heads, jnp.exp2(b - top), 0.0)
    high = a * pltpu.roll(fa, heads, 1) + b * pltpu.roll(fb, heads, 1)
    low = a * pltpu.roll(fa, 2 * heads, 1) + b * pltpu.roll(fb, 2 * heads, 1)
    total = high + pltpu.roll(low, lanes - heads, 1)
    high = total.astype(jnp.bfloat16).astype(jnp.float32)
    low = pltpu.roll(total - high, heads, 1)
    stats = jnp.where(lane < heads, top, jnp.where(lane < 2 * heads, high, low))
    out[:, width:] = stats.astype(out.dtype)
    for h in range(heads):
        part = slice(h * size, (h + 1) * size)
        sum_ = mine[:, part].astype(jnp.float32) * fa[:, h : h + 1]
        sum_ = sum_ + other[:, part].astype(jnp.float32) * fb[:, h : h + 1]
        out[:, part] = sum_.astype(out.dtype)


def local_call(kernel, shape, dtype, name, *arrays):
    vmem = pl.BlockSpec(memory_space=pltpu.VMEM)
    return pl.pallas_call(
        kernel,
        in_specs=[vmem] * len(arrays),
        out_specs=vmem,
        out_shape=pltpu.VMEM(shape, dtype),
        compiler_params=pltpu.CompilerParams(vmem_limit_bytes=16 << 20),
        name=name,
    )(*(here(a) for a in arrays))


def finish_kernel(parts, own, out, *, heads, size):
    peers, count, _ = parts.shape
    width = heads * size
    lane = iota((count, lanes), 1)
    stats = [parts[p, :, width:].astype(jnp.float32) for p in range(peers)] + [own[:, width:]]
    top = stats[0]
    for s in stats[1:]:
        top = jnp.maximum(top, s)
    factors = [jnp.where(lane < heads, jnp.exp2(s - top), 0.0) for s in stats]
    high, low = jnp.zeros_like(top), jnp.zeros_like(top)
    for s, f in zip(stats, factors):
        high = high + s * pltpu.roll(f, heads, 1)
        low = low + s * pltpu.roll(f, 2 * heads, 1)
    total = pltpu.roll(high, lanes - heads, 1) + pltpu.roll(low, lanes - 2 * heads, 1)
    inverse = 1.0 / jnp.where(lane < heads, total, 1.0)
    for h in range(heads):
        part = slice(h * size, (h + 1) * size)
        merged = own[:, part] * factors[peers][:, h : h + 1]
        for p in range(peers):
            merged = merged + parts[p, :, part].astype(jnp.float32) * factors[p][:, h : h + 1]
        row = (merged * inverse[:, h : h + 1]).astype(out.dtype)
        for p in range(peers):
            out[p, :, part] = row


def project_kernel(mine, other, weight, out):
    count = mine.shape[0]
    core = lax.rem(lax.axis_index("seq"), 2)
    first = pl.multiple_of(core * count, count)
    second = pl.multiple_of((1 - core) * count, count)
    out[pl.ds(first, count), :] = f32dot(mine[...], weight[...]).astype(out.dtype)
    out[pl.ds(second, count), :] = f32dot(other[...], weight[...]).astype(out.dtype)


def body(queries, new_keys, new_values, cache_keys, cache_values, parents, kv_lengths, out_weight):
    requests, tree, heads, size = queries.shape
    peers = lax.axis_size("seq")
    head_peers = lax.axis_size("head")
    tokens = requests * tree
    block = cache_keys.shape[1]
    chips = peers // 2
    count = tokens // peers
    width = heads * size
    scale = math.log2(math.e) / math.sqrt(size)
    same_core = [[2 * i + c for i in range(chips)] for c in range(2)]
    kept, arrived, own = cache_parts(
        kv_lengths, parents, queries,
        new_keys.reshape(requests, tree, size), new_values.reshape(requests, tree, size),
        cache_keys.reshape(requests, block, size), cache_values.reshape(requests, block, size),
        peers, scale,
    )
    pair = local_call(
        functools.partial(join_kernel, heads=heads, size=size),
        (tokens // 2, width + lanes), jnp.bfloat16, "join", kept, arrived,
    )
    parts = lax.all_to_all(
        pair.reshape(chips, count, -1), "seq", 0, 0, tiled=True, axis_index_groups=same_core
    )
    share = local_call(
        functools.partial(finish_kernel, heads=heads, size=size),
        (chips, count, width), jnp.bfloat16, "finish", parts, own,
    )
    mine = lax.all_to_all(share, "seq", 0, 0, tiled=True, axis_index_groups=same_core)
    mine = mine.reshape(tokens // 2, width)
    other = lax.ppermute(mine, "seq", [(i, i ^ 1) for i in range(peers)])
    partial = local_call(
        project_kernel, (tokens, out_weight.shape[1]), jnp.bfloat16, "project", mine, other, out_weight
    )
    pieces = lax.all_to_all(
        partial.reshape(head_peers, tokens // head_peers, -1), "head", 0, 0, tiled=True
    )
    return pieces.astype(jnp.float32).sum(axis=0).astype(jnp.bfloat16)


def solution(mesh):
    placed = (
        P(None, None, "head", None),
        P(None, None, "head", None),
        P(None, None, "head", None),
        P(None, "seq", "head", None),
        P(None, "seq", "head", None),
        P(),
        P(),
        P("head", "seq"),
    )
    return jax.shard_map(
        body, mesh=mesh, in_specs=placed, out_specs=P("head", "seq"), check_vma=False
    )
```

time: 76 us -> 64.3 us (0.85); the launches traced: 74.9 us -> 64.1 us
  blocking collectives: 27.4 us -> 43.9 us
  Pallas kernels: 22.8 us -> 11.1 us
  starting transfers between devices: 12.4 us -> 5.89 us
  waiting for transfers between devices: 7.03 us -> 1.16 us
  other arithmetic: 2.33 us -> 0.63 us
  local copies, waits for them, and re-layouts: 2.86 us -> 1.34 us
    all_to_all x1 -> x2, blocking collectives: 13.8 us -> 30.9 us  [the longest x1 17 us: body(): lax.all_to_all(pair.reshape(chips, count, -1), 'seq', 0, 0, tiled=True, a...]
    pallas_call x6 -> x5, Pallas kernels: 22.8 us -> 11.1 us  [the longest x1 6.58 us: cache_parts(): pl.pallas_call(functools.partial(send_kernel, scale=scale, chunk=chunk, p...]
    all_to_all x1 -> x0, waiting for transfers between devices: 5.87 us -> none  [body(): lax.all_to_all(pair.reshape(chips, count, -1), 'seq', 0, 0, tiled=True, a...]
    all_to_all x1 -> x0, starting transfers between devices: 4.35 us -> none  [body(): lax.all_to_all(pair.reshape(chips, count, -1), 'seq', 0, 0, tiled=True, a...]
    ppermute x2, starting transfers between devices: 8.05 us -> 5.89 us  [the longest x1 3.29 us: cache_parts(): arrived = lax.ppermute(sent, 'seq', [(i, i ^ 1) for i in range(peers)])]
    another operation x3 -> x0, other arithmetic: 1.7 us -> none  [the longest x2 1.11 us: at(): return jnp.stack([base, place * block]).astype(jnp.int32)]
    unnamed x8 -> x6, local copies, waits for them, and re-layouts: 2.12 us -> 1.34 us
  transfers between devices with their start and end apart: 3 -> 2, of which waited for: 2 -> 1; matrix products, arithmetic and copies ran while one was open for 2% -> 0% of each run, Pallas kernels for 15% -> 5%
where the time goes in v2:
time: 64.3 us; the launch traced here: 64.1 us
  blocking collectives  43.9 us (68%)
  Pallas kernels  11.1 us (17%)
  starting transfers between devices  5.89 us (9%)
  local copies, waits for them, and re-layouts  1.34 us (2%)
  waiting for transfers between devices  1.16 us (2%)
    all_to_all x1, blocking collectives, body(): lax.all_to_all(pair.reshape(chips, count, -1), 'seq', 0, 0, tiled=True, a...  17 us
    all_to_all x1, blocking collectives, body(): lax.all_to_all(share, 'seq', 0, 0, tiled=True, axis_index_groups=same_core)  13.8 us
    all_to_all x1, blocking collectives, body(): lax.all_to_all(partial.reshape(head_peers, tokens // head_peers, -1), 'he...  13.1 us
    pallas_call x1, Pallas kernels, cache_parts(): pl.pallas_call(functools.partial(send_kernel, scale=scale, chunk=chunk, p...  6.58 us
    pallas_call x1, Pallas kernels, cache_parts(): pl.pallas_call(functools.partial(keep_kernel, scale=scale, chunk=chunk, t...  3.31 us
    ppermute x1, starting transfers between devices, cache_parts(): arrived = lax.ppermute(sent, 'seq', [(i, i ^ 1) for i in range(peers)])  3.29 us
    ppermute x1, starting transfers between devices, body(): other = lax.ppermute(mine, 'seq', [(i, i ^ 1) for i in range(peers)])  2.6 us
    unnamed x6, local copies, waits for them, and re-layouts  1.34 us
  transfers between devices with their start and end apart: 2, of which 1 were waited for; matrix products, arithmetic and copies ran while one was open for 0% of the time, Pallas kernels for 5%

profile of v2, /device:TPU:1, one launch (start us, length us, event | category | flops | bytes accessed | tf_op | source)
XLA Modules:
  0.0 64.1 jit_solution(6107224880451180679)
XLA Ops:
  0.0 0.0 copy-start.1
  0.0 0.7 %copy-done.1 = s32[4,64]{1,0:T(4,128)S(1)} copy-done((s32[4,64]{1,0:T(4,128)S(1)}, s32[4,64]{1,0:T(4,128)}, u32[]{:S(2)}) %copy-start.1) | copy-done | bytes 1048
  0.7 0.0 copy-start.2
  0.7 0.7 %copy-done.2 = s32[4]{0:T(128)S(1)} copy-done((s32[4]{0:T(128)S(1)}, s32[4]{0:T(128)}, u32[]{:S(2)}) %copy-start.2) | copy-done | bytes 40
  1.3 6.6 %send_part.1 = (bf16[128,1152]{1,0:T(8,128)(2,1)S(1)}, f32[8,1152]{1,0:T(8,128)S(1)}, bf16[2,512,128]{2,1,0:T(8,128)(2,1)S(1)}, bf16[2,2048,128]{2,1,0:T(8,128)(2,1)S(1)}, bf16[2,2048,128]{2,1,0:T(8,128)(2,1)S(1)}) custom-call(s32[4]{0:T(128)S(1)} %copy-done.2, s32[4,64]{1,0:T(4,128)S(1)} %copy-done.1, bf16[4,64,8,128]{3,2,1,0:T(8,128)(2,1)} %queries.1, ...), custom_call_target="tpu_custom_call" | custom-call | tf_op jit(solution)/shard_map/send_part/pallas_call | solution.py:186
  7.9 3.3 %collective-permute-start = (bf16[128,1152]{1,0:T(8,128)(2,1)S(1)}, bf16[128,1152]{1,0:T(8,128)(2,1)S(1)}, u32[]{:S(2)}, u32[]{:S(2)}) collective-permute-start(bf16[128,1152]{1,0:T(8,128)(2,1)S(1)} %get-tuple-element.13), channel_id=1, source_target_pairs={{0,8},{8,0},{16,24},{24,16},{32,40},{40,32},{48,56},{56,48},{64,72... | collective-permute-start | bytes 884744 | tf_op jit(solution)/shard_map/ppermute | solution.py:210
  11.2 3.3 %keep_part.1.mine = f32[128,1152]{1,0:T(8,128)S(1)} custom-call(s32[4]{0:T(128)S(1)} %copy-done.2, bf16[2,512,128]{2,1,0:T(8,128)(2,1)S(1)} %get-tuple-element.10.turned, bf16[2,2048,128]{2,1,0:T(8,128)(2,1)S(1)} %get-tuple-element.11.keys, bf16[2,2048,128]{2,1,0:T(8,128)(2,1)S(1)} %get-tuple-element.12.values), custom_call_target="tpu_custom_call" | custom-call | tf_op jit(solution)/shard_map/keep_part/pallas_call | solution.py:211
  14.5 0.0 copy-start
  14.6 0.0 collective-permute-done.other
  14.6 0.5 join.1
  15.1 17.0 %all_to_all.15.parts = bf16[16,8,1152]{2,1,0:T(8,128)(2,1)S(1)} all-to-all(bf16[16,8,1152]{2,1,0:T(8,128)(2,1)S(1)} %bitcast.7), channel_id=1, replica_groups={{0,16,32,48,64,80,96,112,128,144,160,176,192,208,224,240},{8,24,40,56,7..., dimensions={0} | all-to-all | bytes 589824 | tf_op jit(solution)/shard_map/all_to_all | solution.py:312
  32.1 0.3 finish.1
  32.5 13.8 %all_to_all.16 = bf16[16,8,1024]{2,1,0:T(8,128)(2,1)S(1)} all-to-all(bf16[16,8,1024]{2,1,0:T(8,128)(2,1)S(1)} %finish.1), channel_id=1, replica_groups={{0,16,32,48,64,80,96,112,128,144,160,176,192,208,224,240},{8,24,40,56,7..., dimensions={0} | all-to-all | bytes 524288 | tf_op jit(solution)/shard_map/all_to_all | solution.py:319
  46.3 2.6 %collective-permute-start.1 = (bf16[128,1024]{1,0:T(8,128)(2,1)S(1)}, bf16[128,1024]{1,0:T(8,128)(2,1)S(1)}, u32[]{:S(2)}, u32[]{:S(2)}) collective-permute-start(bf16[128,1024]{1,0:T(8,128)(2,1)S(1)} %bitcast.8), channel_id=1, source_target_pairs={{0,8},{8,0},{16,24},{24,16},{32,40},{40,32},{48,56},{56,48},{64,72... | collective-permute-start | bytes 786440 | tf_op jit(solution)/shard_map/ppermute | solution.py:321
  48.9 1.2 %collective-permute-done.1.other = bf16[128,1024]{1,0:T(8,128)(2,1)S(1)} collective-permute-done((bf16[128,1024]{1,0:T(8,128)(2,1)S(1)}, bf16[128,1024]{1,0:T(8,128)(2,1)S(1)}, u32[]{:S(2)}, u32[]{:S(2)}) %collective-permute-start.1) | collective-permute-done | bytes 262176 | tf_op jit(solution)/shard_map/ppermute | solution.py:321
  50.0 0.0 copy-done
  50.0 0.3 project.1
  50.4 13.1 %all_to_all.17 = bf16[8,32,256]{2,1,0:T(8,128)(2,1)S(1)} all-to-all(bf16[8,32,256]{2,1,0:T(8,128)(2,1)S(1)} %bitcast.10), channel_id=1, replica_groups=mesh['seq'=32,'head'=8] {'head'}, dimensions={0} | all-to-all | bytes 262144 | tf_op jit(solution)/shard_map/all_to_all | solution.py:325
  63.5 0.6 reduce_sum.12
Async XLA Ops:
  0.0 0.7 %copy-start.1 = (s32[4,64]{1,0:T(4,128)S(1)}, s32[4,64]{1,0:T(4,128)}, u32[]{:S(2)}) copy-start(s32[4,64]{1,0:T(4,128)} %parents.1) | copy-start | bytes 3076
  0.7 0.7 %copy-start.2 = (s32[4]{0:T(128)S(1)}, s32[4]{0:T(128)}, u32[]{:S(2)}) copy-start(s32[4]{0:T(128)} %lengths.3) | copy-start | bytes 52
  7.9 6.6 %collective-permute-start = (bf16[128,1152]{1,0:T(8,128)(2,1)S(1)}, bf16[128,1152]{1,0:T(8,128)(2,1)S(1)}, u32[]{:S(2)}, u32[]{:S(2)}) collective-permute-start(bf16[128,1152]{1,0:T(8,128)(2,1)S(1)} %get-tuple-element.13), channel_id=1, source_target_pairs={{0,8},{8,0},{16,24},{24,16},{32,40},{40,32},{48,56},{56,48},{64,72... | collective-permute-start | bytes 884744 | tf_op jit(solution)/shard_map/ppermute | solution.py:210
  14.5 35.5 %copy-start = (bf16[1024,256]{1,0:T(8,128)(2,1)S(1)}, bf16[1024,256]{1,0:T(8,128)(2,1)}, u32[]{:S(2)}) copy-start(bf16[1024,256]{1,0:T(8,128)(2,1)} %weight.1) | copy-start | bytes 1572868
  46.3 3.8 %collective-permute-start.1 = (bf16[128,1024]{1,0:T(8,128)(2,1)S(1)}, bf16[128,1024]{1,0:T(8,128)(2,1)S(1)}, u32[]{:S(2)}, u32[]{:S(2)}) collective-permute-start(bf16[128,1024]{1,0:T(8,128)(2,1)S(1)} %bitcast.8), channel_id=1, source_target_pairs={{0,8},{8,0},{16,24},{24,16},{32,40},{40,32},{48,56},{56,48},{64,72... | collective-permute-start | bytes 786440 | tf_op jit(solution)/shard_map/ppermute | solution.py:321

commit v3 on v2

--- a/solution.py
+++ b/solution.py
@@ -29,6 +29,17 @@
 
 def away(array):
     return pltpu.with_memory_space_constraint(array, pltpu.MemorySpace.HBM)
+
+
+def owned(place, requests, tree, peers, head_peers):
+    core, chip = lax.rem(place, 2), lax.div(place, 2)
+    chips = peers // 4
+    y, z = lax.div(chip, chips), lax.rem(chip, chips)
+    tokens = requests * tree
+    rows, count = tokens // head_peers, tokens // peers
+    per = rows // 2 // count
+    token = (core * (head_peers // 2) + lax.div(z, per)) * rows + y * (rows // 2) + lax.rem(z, per) * count
+    return lax.div(token, tree), lax.rem(token, tree)
 
 
 def regroup(count, heads, total, first=0):
@@ -91,20 +102,38 @@
     out[:, width:] = put_stats(top, total[:, size:], count, heads).astype(out.dtype)
 
 
-def draft(turned, keys, values, parent_row, first, out, heads, scale):
-    rows, size = turned.shape
-    count, tree, width = rows // heads, keys.shape[0], heads * size
+def draft_kernel(
+    parents_far, queries, draft_keys, draft_values, out, parents, query, keys, values, sems,
+    *, scale, peers, head_peers,
+):
+    requests, tree, heads, size = queries.shape
+    count, width = out.shape[0], heads * size
+    rows = count * heads
+    request, first = owned(lax.axis_index("seq"), requests, tree, peers, head_peers)
+    first = pl.multiple_of(first, count)
+    copies = [
+        pltpu.make_async_copy(parents_far, parents, sems.at[0]),
+        pltpu.make_async_copy(queries.at[request, pl.ds(first, count)], query, sems.at[1]),
+        pltpu.make_async_copy(draft_keys.at[request], keys, sems.at[2]),
+        pltpu.make_async_copy(draft_values.at[request], values, sems.at[3]),
+    ]
+    for copy in copies:
+        copy.start()
+    for copy in copies:
+        copy.wait()
+    turned = f32dot(regroup(count, heads, count), query[...].reshape(rows, size)).astype(jnp.bfloat16)
+    parent_row = parents[pl.ds(request, 1), :]
     j, i = iota((tree, tree), 0), iota((tree, tree), 1)
     reached = ((parent_row == j) | (i == j)).astype(jnp.bfloat16)
     for repeat in range(max(1, (tree - 1).bit_length())):
         reached = jnp.minimum(f32dot(reached, reached), 1.0).astype(jnp.bfloat16)
     own = iota((count, tree), 1) == iota((count, tree), 0) + first
     allowed = f32dot(own.astype(jnp.bfloat16), reached, dims_last) > 0.5
-    s = f32dot(turned, keys, dims_last).reshape(heads, count, tree)
+    s = f32dot(turned, keys[...], dims_last).reshape(heads, count, tree)
     s = jnp.where(allowed[None], s * scale, lowest).reshape(rows, tree)
     top = jnp.max(s, axis=1, keepdims=True)
     weights = jnp.exp2(s - top).astype(jnp.bfloat16)
-    wide = jnp.concatenate([values, jnp.ones((tree, lanes), jnp.bfloat16)], axis=1)
+    wide = jnp.concatenate([values[...], jnp.ones((tree, lanes), jnp.bfloat16)], axis=1)
     total = f32dot(weights, wide)
     for h in range(heads):
         out[:, h * size : (h + 1) * size] = total[h * count : (h + 1) * count, :size]
@@ -112,25 +141,22 @@
 
 
 def send_kernel(
-    lengths, parents, queries, draft_keys, draft_values, keys, values,
-    sent, own, turned, kept_keys, kept_values,
-    query, left_keys, left_values, left_turned, tree_keys, tree_values, scores, sems,
-    *, scale, chunk, peers,
+    lengths_far, queries, keys, values,
+    sent, turned, kept_keys, kept_values,
+    lengths, query, left_keys, left_values, left_turned, scores, sems,
+    *, scale, chunk,
 ):
     requests, tree, heads, size = queries.shape
     block = keys.shape[1]
     half = requests // 2
-    count = requests * tree // peers
     place = lax.axis_index("seq")
-    core, chip = lax.rem(place, 2), lax.div(place, 2)
+    core = lax.rem(place, 2)
     mine, left = core * half, (1 - core) * half
-    token = chip * count
-    request, first = mine + lax.div(token, tree), lax.rem(token, tree)
 
     copies = [
-        pltpu.make_async_copy(queries, query, sems.at[0]),
-        pltpu.make_async_copy(draft_keys.at[request], tree_keys, sems.at[1]),
-        pltpu.make_async_copy(draft_values.at[request], tree_values, sems.at[2]),
+        pltpu.make_async_copy(lengths_far, lengths, sems.at[0]),
+        pltpu.make_async_copy(queries.at[pl.ds(left, half)], query.at[pl.ds(0, half)], sems.at[1]),
+        pltpu.make_async_copy(queries.at[pl.ds(mine, half)], query.at[pl.ds(half, half)], sems.at[2]),
     ]
     for r in range(half):
         copies.append(pltpu.make_async_copy(keys.at[left + r], left_keys.at[r], sems.at[3 + 2 * r]))
@@ -142,15 +168,13 @@
         copy.start()
 
     spin = regroup(tree, heads, tree)
-    pick = regroup(count, heads, tree, first)
     copies[0].wait()
+    copies[1].wait()
     for r in range(half):
-        left_turned[r] = f32dot(spin, query[left + r].reshape(tree * heads, size)).astype(jnp.bfloat16)
-        turned[r] = f32dot(spin, query[mine + r].reshape(tree * heads, size)).astype(jnp.bfloat16)
-    picked = f32dot(pick, query[request].reshape(tree * heads, size)).astype(jnp.bfloat16)
-    copies[1].wait()
+        left_turned[r] = f32dot(spin, query[r].reshape(tree * heads, size)).astype(jnp.bfloat16)
     copies[2].wait()
-    draft(picked, tree_keys[...], tree_values[...], parents[pl.ds(request, 1), :], first, own, heads, scale)
+    for r in range(half):
+        turned[r] = f32dot(spin, query[half + r].reshape(tree * heads, size)).astype(jnp.bfloat16)
     for r in range(half):
         copies[3 + 2 * r].wait()
         attend(
@@ -161,11 +185,14 @@
     copies[late + 1].wait()
 
 
-def keep_kernel(lengths, turned, keys, values, out, scores, *, scale, chunk, tree):
+def keep_kernel(lengths_far, turned, keys, values, out, lengths, scores, sem, *, scale, chunk, tree):
+    copy = pltpu.make_async_copy(lengths_far, lengths, sem)
+    copy.start()
     half, rows, size = turned.shape
     block = keys.shape[1]
     place = lax.axis_index("seq")
     mine = lax.rem(place, 2) * half
+    copy.wait()
     for r in range(half):
         attend(
             turned.at[r], keys.at[r], values.at[r], lengths[mine + r] - place * block,
@@ -173,56 +200,81 @@
         )
 
 
-def cache_parts(lengths, parents, queries, draft_keys, draft_values, keys, values, peers, scale, chunk=256):
+def draft_part(parents, queries, draft_keys, draft_values, peers, head_peers, scale):
+    requests, tree, heads, size = queries.shape
+    count = requests * tree // peers
+    bf16 = jnp.bfloat16
+    return pl.pallas_call(
+        functools.partial(draft_kernel, scale=scale, peers=peers, head_peers=head_peers),
+        in_specs=[pl.BlockSpec(memory_space=pltpu.HBM)] * 4,
+        out_specs=pl.BlockSpec(memory_space=pltpu.VMEM),
+        out_shape=pltpu.VMEM((count, heads * size + lanes), jnp.float32),
+        scratch_shapes=[
+            pltpu.VMEM((requests, tree), jnp.int32),
+            pltpu.VMEM((count, heads, size), bf16),
+            pltpu.VMEM((tree, size), bf16),
+            pltpu.VMEM((tree, size), bf16),
+            pltpu.SemaphoreType.DMA((4,)),
+        ],
+        compiler_params=pltpu.CompilerParams(vmem_limit_bytes=8 << 20),
+        name="draft_part",
+    )(*(away(a) for a in (parents, queries, draft_keys, draft_values)))
+
+
+def cache_parts(lengths, queries, keys, values, peers, scale, chunk=256):
     requests, tree, heads, size = queries.shape
     block = keys.shape[1]
     half = requests // 2
     rows, width = tree * heads, heads * size + lanes
-    count = requests * tree // peers
-    smem, vmem, far = (pl.BlockSpec(memory_space=m) for m in (pltpu.SMEM, pltpu.VMEM, pltpu.HBM))
+    vmem, far = (pl.BlockSpec(memory_space=m) for m in (pltpu.VMEM, pltpu.HBM))
     scores = pltpu.VMEM((rows, block), jnp.float32)
     bf16 = jnp.bfloat16
     limit = pltpu.CompilerParams(vmem_limit_bytes=24 << 20)
-    sent, own, turned, kept_keys, kept_values = pl.pallas_call(
-        functools.partial(send_kernel, scale=scale, chunk=chunk, peers=peers),
-        in_specs=[smem, vmem, far, far, far, far, far],
-        out_specs=[vmem] * 5,
+    sent, turned, kept_keys, kept_values = pl.pallas_call(
+        functools.partial(send_kernel, scale=scale, chunk=chunk),
+        in_specs=[far] * 4,
+        out_specs=[vmem] * 4,
         out_shape=[
             pltpu.VMEM((half * tree, width), bf16),
-            pltpu.VMEM((count, width), jnp.float32),
             pltpu.VMEM((half, rows, size), bf16),
             pltpu.VMEM((half, block, size), bf16),
             pltpu.VMEM((half, block, size), bf16),
         ],
         scratch_shapes=[
+            pltpu.SMEM((requests,), jnp.int32),
             pltpu.VMEM((requests, tree, heads, size), bf16),
             pltpu.VMEM((half, block, size), bf16),
             pltpu.VMEM((half, block, size), bf16),
             pltpu.VMEM((half, rows, size), bf16),
-            pltpu.VMEM((tree, size), bf16),
-            pltpu.VMEM((tree, size), bf16),
             scores,
             pltpu.SemaphoreType.DMA((5 + 2 * half,)),
         ],
         compiler_params=limit,
         name="send_part",
-    )(lengths, parents, *(away(a) for a in (queries, draft_keys, draft_values, keys, values)))
+    )(*(away(a) for a in (lengths, queries, keys, values)))
     arrived = lax.ppermute(sent, "seq", [(i, i ^ 1) for i in range(peers)])
     kept = pl.pallas_call(
         functools.partial(keep_kernel, scale=scale, chunk=chunk, tree=tree),
-        in_specs=[smem, vmem, vmem, vmem],
+        in_specs=[far, vmem, vmem, vmem],
         out_specs=vmem,
         out_shape=pltpu.VMEM((half * tree, width), jnp.float32),
-        scratch_shapes=[scores],
+        scratch_shapes=[pltpu.SMEM((requests,), jnp.int32), scores, pltpu.SemaphoreType.DMA],
         compiler_params=limit,
         name="keep_part",
-    )(lengths, here(turned), here(kept_keys), here(kept_values))
-    return kept, arrived, own
-
-
-def join_kernel(mine, other, out, *, heads, size):
+    )(away(lengths), here(turned), here(kept_keys), here(kept_values))
+    return kept, arrived
+
+
+def join_kernel(mine, other, out, *, heads, size, order):
     count = mine.shape[0]
     width = heads * size
+    each = out.shape[1]
+
+    def put(value, lane_slice):
+        value = value.astype(out.dtype)
+        for i, first in enumerate(order):
+            out[i, :, lane_slice] = value[first : first + each]
+
     a, b = mine[:, width:].astype(jnp.float32), other[:, width:].astype(jnp.float32)
     lane = iota((count, lanes), 1)
     top = jnp.maximum(a, b)
@@ -234,12 +286,12 @@
     high = total.astype(jnp.bfloat16).astype(jnp.float32)
     low = pltpu.roll(total - high, heads, 1)
     stats = jnp.where(lane < heads, top, jnp.where(lane < 2 * heads, high, low))
-    out[:, width:] = stats.astype(out.dtype)
+    put(stats, slice(width, width + lanes))
     for h in range(heads):
         part = slice(h * size, (h + 1) * size)
         sum_ = mine[:, part].astype(jnp.float32) * fa[:, h : h + 1]
         sum_ = sum_ + other[:, part].astype(jnp.float32) * fb[:, h : h + 1]
-        out[:, part] = sum_.astype(out.dtype)
+        put(sum_, part)
 
 
 def local_call(kernel, shape, dtype, name, *arrays):
@@ -275,17 +327,19 @@
         for p in range(peers):
             merged = merged + parts[p, :, part].astype(jnp.float32) * factors[p][:, h : h + 1]
         row = (merged * inverse[:, h : h + 1]).astype(out.dtype)
-        for p in range(peers):
+        for p in range(out.shape[0]):
             out[p, :, part] = row
 
 
-def project_kernel(mine, other, weight, out):
-    count = mine.shape[0]
-    core = lax.rem(lax.axis_index("seq"), 2)
-    first = pl.multiple_of(core * count, count)
-    second = pl.multiple_of((1 - core) * count, count)
-    out[pl.ds(first, count), :] = f32dot(mine[...], weight[...]).astype(out.dtype)
-    out[pl.ds(second, count), :] = f32dot(other[...], weight[...]).astype(out.dtype)
+def project_kernel(mine, other, weight, next_weight, out, *, head_peers):
+    place = lax.axis_index("seq")
+    core, y = lax.rem(place, 2), lax.div(place, lax.axis_size("seq") // 2)
+    blocks = head_peers // 2
+    rows = out.shape[1]
+    for array, half in ((mine, core), (other, 1 - core)):
+        for columns, at in ((weight, y), (next_weight, 1 - y)):
+            part = f32dot(array[...], columns[...]).astype(out.dtype)
+            out[pl.ds(at * head_peers + half * blocks, blocks)] = part.reshape(blocks, rows, -1)
 
 
 def body(queries, new_keys, new_values, cache_keys, cache_values, parents, kv_lengths, out_weight):
@@ -294,38 +348,50 @@
     head_peers = lax.axis_size("head")
     tokens = requests * tree
     block = cache_keys.shape[1]
-    chips = peers // 2
+    chips, line = peers // 2, peers // 4
     count = tokens // peers
     width = heads * size
+    rows = tokens // head_peers
     scale = math.log2(math.e) / math.sqrt(size)
     same_core = [[2 * i + c for i in range(chips)] for c in range(2)]
-    kept, arrived, own = cache_parts(
-        kv_lengths, parents, queries,
-        new_keys.reshape(requests, tree, size), new_values.reshape(requests, tree, size),
+    same_line = [[2 * (y * line + z) + c for z in range(line)] for y in range(2) for c in range(2)]
+    same_plane = [
+        [(2 * (y * line + z) + c) * head_peers + h for y in range(2) for h in range(head_peers)]
+        for z in range(line) for c in range(2)
+    ]
+    per = rows // 2 // count
+    order = [(z // per) * rows + y * (rows // 2) + (z % per) * count for y in range(2) for z in range(line)]
+    kept, arrived = cache_parts(
+        kv_lengths, queries,
         cache_keys.reshape(requests, block, size), cache_values.reshape(requests, block, size),
         peers, scale,
     )
+    next_weight = lax.ppermute(out_weight, "seq", [(i, (i + chips) % peers) for i in range(peers)])
     pair = local_call(
-        functools.partial(join_kernel, heads=heads, size=size),
-        (tokens // 2, width + lanes), jnp.bfloat16, "join", kept, arrived,
-    )
-    parts = lax.all_to_all(
-        pair.reshape(chips, count, -1), "seq", 0, 0, tiled=True, axis_index_groups=same_core
+        functools.partial(join_kernel, heads=heads, size=size, order=order),
+        (chips, count, width + lanes), jnp.bfloat16, "join", kept, arrived,
+    )
+    parts = lax.all_to_all(pair, "seq", 0, 0, tiled=True, axis_index_groups=same_core)
+    own = draft_part(
+        parents, queries,
+        new_keys.reshape(requests, tree, size), new_values.reshape(requests, tree, size),
+        peers, head_peers, scale,
     )
     share = local_call(
         functools.partial(finish_kernel, heads=heads, size=size),
-        (chips, count, width), jnp.bfloat16, "finish", parts, own,
-    )
-    mine = lax.all_to_all(share, "seq", 0, 0, tiled=True, axis_index_groups=same_core)
-    mine = mine.reshape(tokens // 2, width)
+        (line, count, width), jnp.bfloat16, "finish", parts, own,
+    )
+    mine = lax.all_to_all(share, "seq", 0, 0, tiled=True, axis_index_groups=same_line)
+    mine = mine.reshape(line * count, width)
     other = lax.ppermute(mine, "seq", [(i, i ^ 1) for i in range(peers)])
     partial = local_call(
-        project_kernel, (tokens, out_weight.shape[1]), jnp.bfloat16, "project", mine, other, out_weight
-    )
-    pieces = lax.all_to_all(
-        partial.reshape(head_peers, tokens // head_peers, -1), "head", 0, 0, tiled=True
-    )
-    return pieces.astype(jnp.float32).sum(axis=0).astype(jnp.bfloat16)
+        functools.partial(project_kernel, head_peers=head_peers),
+        (2 * head_peers, rows // 2, out_weight.shape[1]), jnp.bfloat16, "project",
+        mine, other, out_weight, next_weight,
+    )
+    pieces = lax.all_to_all(partial, ("seq", "head"), 0, 0, tiled=True, axis_index_groups=same_plane)
+    pieces = pieces.reshape(2, head_peers, rows // 2, -1).astype(jnp.float32).sum(axis=1)
+    return pieces.reshape(rows, -1).astype(jnp.bfloat16)
 
 
 def solution(mesh):

time: 64.3 us -> 61.6 us (0.958)
  blocking collectives: 43.9 us -> 25.8 us
  starting transfers between devices: 5.89 us -> 15.1 us
  waiting for transfers between devices: 1.16 us -> 7.23 us
  local copies, waits for them, and re-layouts: 1.34 us -> 0.01 us
  Pallas kernels: 11.1 us -> 12.4 us
    all_to_all x3 -> x2, blocking collectives: 43.9 us -> 25.8 us  [the longest x1 13.3 us: body(): lax.all_to_all(partial, ('seq', 'head'), 0, 0, tiled=True, axis_index_gro...]
    all_to_all x0 -> x1, starting transfers between devices: none -> 7.6 us  [body(): lax.all_to_all(pair, 'seq', 0, 0, tiled=True, axis_index_groups=same_core)]
    all_to_all x0 -> x1, waiting for transfers between devices: none -> 6.24 us  [body(): lax.all_to_all(pair, 'seq', 0, 0, tiled=True, axis_index_groups=same_core)]
    ppermute x0 -> x1, starting transfers between devices: none -> 1.45 us  [body(): lax.ppermute(out_weight, 'seq', [(i, (i + chips) % peers) for i in range(...]
    unnamed x6 -> x2, local copies, waits for them, and re-layouts: 1.34 us -> 0.01 us
    pallas_call x3, Pallas kernels: 1.15 us -> 2 us  [local_call(): pl.pallas_call(kernel, in_specs=[vmem] * len(arrays), out_specs=vmem, out...]
    pallas_call x1 -> x2, Pallas kernels: 6.58 us -> 6.9 us  [the longest x1 5 us: cache_parts(): pl.pallas_call(functools.partial(send_kernel, scale=scale, chunk=chunk),...]
  transfers between devices with their start and end apart: 2 -> 4, of which waited for: 1 -> 2; matrix products, arithmetic and copies ran while one was open for 0% -> 0% of each run, Pallas kernels for 5% -> 9%
where the time goes in v3:
time: 61.6 us; the launch traced here: 61.2 us
  blocking collectives  25.8 us (42%)
  starting transfers between devices  15.1 us (25%)
  Pallas kernels  12.4 us (20%)
  waiting for transfers between devices  7.23 us (12%)
  other arithmetic  0.63 us (1%)
    all_to_all x1, blocking collectives, body(): lax.all_to_all(partial, ('seq', 'head'), 0, 0, tiled=True, axis_index_gro...  13.3 us
    all_to_all x1, blocking collectives, body(): lax.all_to_all(share, 'seq', 0, 0, tiled=True, axis_index_groups=same_line)  12.5 us
    all_to_all x1, starting transfers between devices, body(): lax.all_to_all(pair, 'seq', 0, 0, tiled=True, axis_index_groups=same_core)  7.6 us
    all_to_all x1, waiting for transfers between devices, body(): lax.all_to_all(pair, 'seq', 0, 0, tiled=True, axis_index_groups=same_core)  6.24 us
    pallas_call x1, Pallas kernels, cache_parts(): pl.pallas_call(functools.partial(send_kernel, scale=scale, chunk=chunk),...  5 us
    pallas_call x1, Pallas kernels, cache_parts(): pl.pallas_call(functools.partial(keep_kernel, scale=scale, chunk=chunk, t...  3.51 us
    ppermute x1, starting transfers between devices, cache_parts(): arrived = lax.ppermute(sent, 'seq', [(i, i ^ 1) for i in range(peers)])  3.29 us
    ppermute x1, starting transfers between devices, body(): other = lax.ppermute(mine, 'seq', [(i, i ^ 1) for i in range(peers)])  2.78 us
  transfers between devices with their start and end apart: 4, of which 2 were waited for; matrix products, arithmetic and copies ran while one was open for 0% of the time, Pallas kernels for 9%

profile of v3, /device:TPU:1, one launch (start us, length us, event | category | flops | bytes accessed | tf_op | source)
XLA Modules:
  0.0 61.2 jit_solution(4153339950802702218)
XLA Ops:
  0.0 5.0 %send_part.1 = (bf16[128,1152]{1,0:T(8,128)(2,1)S(1)}, bf16[2,512,128]{2,1,0:T(8,128)(2,1)S(1)}, bf16[2,2048,128]{2,1,0:T(8,128)(2,1)S(1)}, bf16[2,2048,128]{2,1,0:T(8,128)(2,1)S(1)}) custom-call(s32[4]{0:T(128)} %lengths_far.3, bf16[4,64,8,128]{3,2,1,0:T(8,128)(2,1)} %queries.3, bf16[4,2048,128]{2,1,0:T(8,128)(2,1)} %bitcast.10, bf16[4,2048,128]{2,1,0:T(8,128)(2,1)} %bitcast.11), custom_call_target="tpu_custom_call" | custom-call | tf_op jit(solution)/shard_map/send_part/pallas_call | solution.py:233
  5.0 3.3 %collective-permute-start = (bf16[128,1152]{1,0:T(8,128)(2,1)S(1)}, bf16[128,1152]{1,0:T(8,128)(2,1)S(1)}, u32[]{:S(2)}, u32[]{:S(2)}) collective-permute-start(bf16[128,1152]{1,0:T(8,128)(2,1)S(1)} %get-tuple-element.12), channel_id=1, source_target_pairs={{0,8},{8,0},{16,24},{24,16},{32,40},{40,32},{48,56},{56,48},{64,72... | collective-permute-start | bytes 884744 | tf_op jit(solution)/shard_map/ppermute | solution.py:255
  8.3 0.0 copy-start
  8.3 3.5 %keep_part.1.mine = f32[128,1152]{1,0:T(8,128)S(1)} custom-call(s32[4]{0:T(128)} %lengths_far.3, bf16[2,512,128]{2,1,0:T(8,128)(2,1)S(1)} %get-tuple-element.9.turned, bf16[2,2048,128]{2,1,0:T(8,128)(2,1)S(1)} %get-tuple-element.10.keys, bf16[2,2048,128]{2,1,0:T(8,128)(2,1)S(1)} %get-tuple-element.11.values), custom_call_target="tpu_custom_call" | custom-call | tf_op jit(solution)/shard_map/keep_part/pallas_call | solution.py:256
  11.8 0.0 collective-permute-done.other
  11.8 1.2 %join.1 = bf16[16,8,1152]{2,1,0:T(8,128)(2,1)} custom-call(f32[128,1152]{1,0:T(8,128)S(1)} %keep_part.1.mine, bf16[128,1152]{1,0:T(8,128)(2,1)S(1)} %collective-permute-done.other), custom_call_target="tpu_custom_call" | custom-call | tf_op jit(solution)/shard_map/join/pallas_call | solution.py:299
  13.0 7.6 %all-to-all-start = ((bf16[16,8,1152]{2,1,0:T(8,128)(2,1)}), bf16[16,8,1152]{2,1,0:T(8,128)(2,1)S(1)}, u32[]{:S(2)}, u32[]{:S(2)}) async-start(bf16[16,8,1152]{2,1,0:T(8,128)(2,1)} %join.1), calls=%async_computation | async-start | bytes 589824 | tf_op jit(solution)/shard_map/all_to_all | solution.py:374
  20.7 0.0 copy-done
  20.7 1.5 %collective-permute-start.2 = (bf16[1024,256]{1,0:T(8,128)(2,1)S(1)}, bf16[1024,256]{1,0:T(8,128)(2,1)S(1)}, u32[]{:S(2)}, u32[]{:S(2)}) collective-permute-start(bf16[1024,256]{1,0:T(8,128)(2,1)S(1)} %copy-done), channel_id=1, source_target_pairs={{0,128},{8,136},{16,144},{24,152},{32,160},{40,168},{48,176},{56,1... | collective-permute-start | bytes 1572872 | tf_op jit(solution)/shard_map/ppermute | solution.py:369
  22.1 1.9 %draft_part.1.own = f32[8,1152]{1,0:T(8,128)S(1)} custom-call(s32[4,64]{1,0:T(4,128)} %parents_far.1, bf16[4,64,8,128]{3,2,1,0:T(8,128)(2,1)} %queries.3, bf16[4,64,128]{2,1,0:T(8,128)(2,1)} %bitcast.12, bf16[4,64,128]{2,1,0:T(8,128)(2,1)} %bitcast.13), custom_call_target="tpu_custom_call" | custom-call | tf_op jit(solution)/shard_map/draft_part/pallas_call | solution.py:207
  24.0 6.2 %all-to-all-done.parts = bf16[16,8,1152]{2,1,0:T(8,128)(2,1)S(1)} async-done(((bf16[16,8,1152]{2,1,0:T(8,128)(2,1)}), bf16[16,8,1152]{2,1,0:T(8,128)(2,1)S(1)}, u32[]{:S(2)}, u32[]{:S(2)}) %all-to-all-start) | async-done | bytes 294944 | tf_op jit(solution)/shard_map/all_to_all | solution.py:374
  30.3 0.3 finish.1
  30.6 12.5 %all_to_all.15 = bf16[8,8,1024]{2,1,0:T(8,128)(2,1)S(1)} all-to-all(bf16[8,8,1024]{2,1,0:T(8,128)(2,1)S(1)} %finish.1), channel_id=1, replica_groups={{0,16,32,48,64,80,96,112},{8,24,40,56,72,88,104,120},{128,144,160,176,1..., dimensions={0} | all-to-all | bytes 262144 | tf_op jit(solution)/shard_map/all_to_all | solution.py:384
  43.0 2.8 %collective-permute-start.1 = (bf16[64,1024]{1,0:T(8,128)(2,1)S(1)}, bf16[64,1024]{1,0:T(8,128)(2,1)S(1)}, u32[]{:S(2)}, u32[]{:S(2)}) collective-permute-start(bf16[64,1024]{1,0:T(8,128)(2,1)S(1)} %bitcast.8), channel_id=1, source_target_pairs={{0,8},{8,0},{16,24},{24,16},{32,40},{40,32},{48,56},{56,48},{64,72... | collective-permute-start | bytes 393224 | tf_op jit(solution)/shard_map/ppermute | solution.py:386
  45.8 0.0 collective-permute-done.2.next_weight
  45.8 1.0 %collective-permute-done.1.other = bf16[64,1024]{1,0:T(8,128)(2,1)S(1)} collective-permute-done((bf16[64,1024]{1,0:T(8,128)(2,1)S(1)}, bf16[64,1024]{1,0:T(8,128)(2,1)S(1)}, u32[]{:S(2)}, u32[]{:S(2)}) %collective-permute-start.1) | collective-permute-done | bytes 131104 | tf_op jit(solution)/shard_map/ppermute | solution.py:386
  46.8 0.5 project.1
  47.3 13.3 %all_to_all.16 = bf16[16,16,256]{2,1,0:T(8,128)(2,1)S(1)} all-to-all(bf16[16,16,256]{2,1,0:T(8,128)(2,1)S(1)} %project.1), channel_id=1, replica_groups={{0,1,2,3,4,5,6,7,128,129,130,131,132,133,134,135},{8,9,10,11,12,13,14,1..., dimensions={0} | all-to-all | bytes 262144 | tf_op jit(solution)/shard_map/all_to_all | solution.py:392
  60.6 0.6 %bitcast_reduce_fusion = bf16[2,16,256]{2,1,0:T(8,128)(2,1)} fusion(bf16[16,16,256]{2,1,0:T(8,128)(2,1)S(1)} %all_to_all.16), kind=kLoop, calls=%fused_computation | loop fusion | flops 57344 | bytes 147456 | tf_op jit(solution)/shard_map/reduce_sum | solution.py:393
Async XLA Ops:
  5.0 6.8 %collective-permute-start = (bf16[128,1152]{1,0:T(8,128)(2,1)S(1)}, bf16[128,1152]{1,0:T(8,128)(2,1)S(1)}, u32[]{:S(2)}, u32[]{:S(2)}) collective-permute-start(bf16[128,1152]{1,0:T(8,128)(2,1)S(1)} %get-tuple-element.12), channel_id=1, source_target_pairs={{0,8},{8,0},{16,24},{24,16},{32,40},{40,32},{48,56},{56,48},{64,72... | collective-permute-start | bytes 884744 | tf_op jit(solution)/shard_map/ppermute | solution.py:255
  8.3 12.4 %copy-start = (bf16[1024,256]{1,0:T(8,128)(2,1)S(1)}, bf16[1024,256]{1,0:T(8,128)(2,1)}, u32[]{:S(2)}) copy-start(bf16[1024,256]{1,0:T(8,128)(2,1)} %weight.1) | copy-start | bytes 1572868
  13.0 17.2 %all-to-all-start = ((bf16[16,8,1152]{2,1,0:T(8,128)(2,1)}), bf16[16,8,1152]{2,1,0:T(8,128)(2,1)S(1)}, u32[]{:S(2)}, u32[]{:S(2)}) async-start(bf16[16,8,1152]{2,1,0:T(8,128)(2,1)} %join.1), calls=%async_computation | async-start | bytes 589824 | tf_op jit(solution)/shard_map/all_to_all | solution.py:374
  20.7 25.2 %collective-permute-start.2 = (bf16[1024,256]{1,0:T(8,128)(2,1)S(1)}, bf16[1024,256]{1,0:T(8,128)(2,1)S(1)}, u32[]{:S(2)}, u32[]{:S(2)}) collective-permute-start(bf16[1024,256]{1,0:T(8,128)(2,1)S(1)} %copy-done), channel_id=1, source_target_pairs={{0,128},{8,136},{16,144},{24,152},{32,160},{40,168},{48,176},{56,1... | collective-permute-start | bytes 1572872 | tf_op jit(solution)/shard_map/ppermute | solution.py:369
  43.0 3.8 %collective-permute-start.1 = (bf16[64,1024]{1,0:T(8,128)(2,1)S(1)}, bf16[64,1024]{1,0:T(8,128)(2,1)S(1)}, u32[]{:S(2)}, u32[]{:S(2)}) collective-permute-start(bf16[64,1024]{1,0:T(8,128)(2,1)S(1)} %bitcast.8), channel_id=1, source_target_pairs={{0,8},{8,0},{16,24},{24,16},{32,40},{40,32},{48,56},{56,48},{64,72... | collective-permute-start | bytes 393224 | tf_op jit(solution)/shard_map/ppermute | solution.py:386

commit v4 on v3

v4 whole, which is shorter than its diff:
```python
import functools
import math

import jax
import jax.numpy as jnp
from jax import lax
from jax.experimental import pallas as pl
from jax.experimental.pallas import tpu as pltpu
from jax.sharding import PartitionSpec as P


lowest = -1e30
lanes = 128
dims_last = (((1,), (1,)), ((), ()))
dims_mid = (((1,), (0,)), ((), ()))
on_chip = pltpu.MemorySpace.VMEM


def iota(shape, dim):
    return lax.broadcasted_iota(jnp.int32, shape, dim)


def f32dot(a, b, dims=dims_mid):
    return lax.dot_general(a, b, dims, preferred_element_type=jnp.float32)


def here(array):
    return pltpu.with_memory_space_constraint(array, on_chip)


def away(array):
    return pltpu.with_memory_space_constraint(array, pltpu.MemorySpace.HBM)


def owned(place, requests, tree, peers, head_peers):
    core, chip = lax.rem(place, 2), lax.div(place, 2)
    chips = peers // 4
    y, z = lax.div(chip, chips), lax.rem(chip, chips)
    tokens = requests * tree
    rows, count = tokens // head_peers, tokens // peers
    per = rows // 2 // count
    token = (core * (head_peers // 2) + lax.div(z, per)) * rows + y * (rows // 2) + lax.rem(z, per) * count
    return lax.div(token, tree), lax.rem(token, tree)


def store_partial(top, out, scratch, heads, some=None):
    acc, sums, peak = scratch
    rows, size = acc.shape
    count, width = rows // heads, heads * size
    peak[...] = jnp.broadcast_to(top, (rows, lanes))
    lane = iota((count, lanes), 1)
    stats = jnp.zeros((count, lanes), jnp.float32)

    def kept(value, other):
        return value if some is None else jnp.where(some, value, other)

    for h in range(heads):
        mine = pl.ds(h, count, heads)
        out[:, h * size : (h + 1) * size] = kept(acc[mine, :], 0.0).astype(out.dtype)
        whole = kept(sums[mine, :], 0.0)
        high = whole.astype(jnp.bfloat16).astype(jnp.float32)
        stats = jnp.where(lane == h, kept(peak[mine, :], lowest), stats)
        stats = jnp.where(lane == heads + h, high, stats)
        stats = jnp.where(lane == 2 * heads + h, whole - high, stats)
    out[:, width:] = stats.astype(out.dtype)


def score(query, keys, valid, scores, scale, chunk, halves=2):
    rows, block = scores.shape
    part_rows = rows // halves
    best = [None] * halves
    for c in range(block // chunk):
        where = slice(c * chunk, (c + 1) * chunk)
        allowed = iota((1, chunk), 1) + c * chunk < valid
        for g in range(halves):
            mine = slice(g * part_rows, (g + 1) * part_rows)
            part = f32dot(query[mine], keys[where], dims_last)
            part = jnp.where(allowed, part, lowest)
            scores[mine, where] = part
            for j in range(chunk // lanes):
                piece = part[:, j * lanes : (j + 1) * lanes]
                best[g] = piece if best[g] is None else jnp.maximum(best[g], piece)
    tops = []
    for g in range(halves):
        top = jnp.max(best[g], axis=1, keepdims=True) * scale
        tops.append(top.astype(jnp.bfloat16).astype(jnp.float32))
    return tops


def gather_values(scores, values, tops, scratch, scale, chunk):
    acc, sums, _ = scratch
    rows, block = scores.shape
    size = acc.shape[1]
    halves = len(tops)
    part_rows = rows // halves
    added_up = [None] * halves
    for c in range(block // chunk):
        where = slice(c * chunk, (c + 1) * chunk)
        wide = jnp.concatenate([values[where], jnp.ones((chunk, lanes), jnp.bfloat16)], axis=1)
        for g in range(halves):
            mine = slice(g * part_rows, (g + 1) * part_rows)
            weights = jnp.exp2(scores[mine, where] * scale - tops[g]).astype(jnp.bfloat16)
            added = f32dot(weights, wide)
            added_up[g] = added if added_up[g] is None else added_up[g] + added
    for g in range(halves):
        mine = slice(g * part_rows, (g + 1) * part_rows)
        acc[mine, :] = added_up[g][:, :size]
        sums[mine, :] = added_up[g][:, size:]


def attend(
    query, keys, values, valids, out, scratch, tree, heads, scale, chunk, beside=None
):
    scores, *partial = scratch
    number = query.shape[0]
    tops = []
    for r in range(number):
        if r == number - 1 and beside is not None:
            beside()
        tops.append(score(query.at[r], keys.at[r], valids[r], scores.at[r], scale, chunk))
    for r in range(number):
        gather_values(scores.at[r], values.at[r], tops[r], [a.at[r] for a in partial], scale, chunk)
    for r in range(number):
        top = jnp.concatenate(tops[r], axis=0)
        store_partial(top, out.at[pl.ds(r * tree, tree)], [a.at[r] for a in partial], heads, valids[r] > 0)


def draft(query, keys, values, parent_row, first, out, partial, heads, scale):
    rows, size = query.shape
    tree = keys.shape[0]
    count = rows // heads
    acc, sums, _ = partial
    j, i = iota((tree, tree), 0), iota((tree, tree), 1)
    reached = ((parent_row == j) | (i == j)).astype(jnp.bfloat16)
    for _ in range(max(1, (tree - 1).bit_length())):
        reached = jnp.minimum(f32dot(reached, reached), 1.0).astype(jnp.bfloat16)
    own = iota((count, tree), 1) == iota((count, tree), 0) + first
    allowed = f32dot(own.astype(jnp.bfloat16), reached, dims_last) > 0.5
    s = f32dot(query[...], keys[...], dims_last).reshape(count, heads, tree)
    s = jnp.where(allowed[:, None, :], s * scale, lowest).reshape(rows, tree)
    top = jnp.max(s, axis=1, keepdims=True)
    weights = jnp.exp2(s - top).astype(jnp.bfloat16)
    wide = jnp.concatenate([values[...], jnp.ones((tree, lanes), jnp.bfloat16)], axis=1)
    total = f32dot(weights, wide)
    acc[...] = total[:, :size]
    sums[...] = total[:, size:]
    store_partial(top, out, partial, heads)


def send_kernel(
    lengths_far, parents_far, queries, draft_keys, draft_values, keys, values,
    sent, own, lengths, kept_query, kept_keys, kept_values,
    parents, own_query, tree_keys, tree_values, own_acc, own_sums, own_peak,
    query, left_keys, left_values, scores, acc, sums, peak, sems,
    *, scale, chunk, tree, heads, peers, head_peers,
):
    block = keys.shape[1]
    requests = queries.shape[0]
    half = requests // 2
    own_rows = own_query.shape[0]
    place = lax.axis_index("seq")
    core = lax.rem(place, 2)
    mine, left = core * half, (1 - core) * half
    request, first = owned(place, requests, tree, peers, head_peers)
    own_first = pl.multiple_of(first * heads, own_rows)

    pairs = [(lengths_far, lengths), (queries.at[pl.ds(left, half)], query)]
    pairs += [(keys.at[left], left_keys.at[0]), (parents_far, parents)]
    pairs += [(queries.at[request, pl.ds(own_first, own_rows)], own_query)]
    pairs += [(draft_keys.at[request], tree_keys), (draft_values.at[request], tree_values)]
    pairs += [(keys.at[left + r], left_keys.at[r]) for r in range(1, half)]
    pairs += [(values.at[left + r], left_values.at[r]) for r in range(half)]
    late = len(pairs)
    pairs += [(queries.at[pl.ds(mine, half)], kept_query)]
    pairs += [(keys.at[pl.ds(mine, half)], kept_keys), (values.at[pl.ds(mine, half)], kept_values)]
    copies = [pltpu.make_async_copy(a, b, sems.at[i]) for i, (a, b) in enumerate(pairs)]
    for copy in copies:
        copy.start()
    early = 3
    for copy in copies[:early]:
        copy.wait()

    def rest():
        for copy in copies[early:late]:
            copy.wait()
        draft(
            own_query, tree_keys, tree_values, parents[pl.ds(request, 1), :], first, own,
            (own_acc, own_sums, own_peak), heads, scale,
        )

    attend(
        query, left_keys, left_values, [lengths[left + r] - place * block for r in range(half)],
        sent, (scores, acc, sums, peak), tree, heads, scale, chunk,
        rest,
    )
    for copy in copies[late:]:
        copy.wait()


def keep_kernel(lengths, query, keys, values, out, scores, acc, sums, peak, *, scale, chunk, tree, heads):
    half = query.shape[0]
    block = keys.shape[1]
    place = lax.axis_index("seq")
    mine = lax.rem(place, 2) * half
    attend(
        query, keys, values, [lengths[mine + r] - place * block for r in range(half)],
        out, (scores, acc, sums, peak), tree, heads, scale, chunk,
    )


def partial_scratch(*shape):
    return [pltpu.VMEM((*shape, n), jnp.float32) for n in (lanes, lanes, lanes)]


def cache_parts(lengths, parents, queries, draft_keys, draft_values, keys, values, heads, peers, head_peers, scale):
    requests, rows, size = queries.shape
    block, tree = keys.shape[1], draft_keys.shape[1]
    half = requests // 2
    count = requests * tree // peers
    width = heads * size + lanes
    vmem, far, smem = (pl.BlockSpec(memory_space=m) for m in (pltpu.VMEM, pltpu.HBM, pltpu.SMEM))
    working = [pltpu.VMEM((half, rows, block), jnp.float32), *partial_scratch(half, rows)]
    bf16 = jnp.bfloat16
    limit = pltpu.CompilerParams(vmem_limit_bytes=32 << 20)
    settings = dict(scale=scale, chunk=256, tree=tree, heads=heads)
    sent, own, known, kept_query, kept_keys, kept_values = pl.pallas_call(
        functools.partial(send_kernel, peers=peers, head_peers=head_peers, **settings),
        in_specs=[far] * 7,
        out_specs=[vmem, vmem, smem, vmem, vmem, vmem],
        out_shape=[
            pltpu.VMEM((half * tree, width), bf16),
            pltpu.VMEM((count, width), jnp.float32),
            pltpu.SMEM((requests,), jnp.int32),
            pltpu.VMEM((half, rows, size), bf16),
            pltpu.VMEM((half, block, size), bf16),
            pltpu.VMEM((half, block, size), bf16),
        ],
        scratch_shapes=[
            pltpu.VMEM((requests, tree), jnp.int32),
            pltpu.VMEM((count * heads, size), bf16),
            pltpu.VMEM((tree, size), bf16),
            pltpu.VMEM((tree, size), bf16),
            *partial_scratch(count * heads),
            pltpu.VMEM((half, rows, size), bf16),
            pltpu.VMEM((half, block, size), bf16),
            pltpu.VMEM((half, block, size), bf16),
            *working,
            pltpu.SemaphoreType.DMA((9 + 2 * half,)),
        ],
        compiler_params=limit,
        name="send_part",
    )(*(away(a) for a in (lengths, parents, queries, draft_keys, draft_values, keys, values)))
    arrived = lax.ppermute(sent, "seq", [(i, i ^ 1) for i in range(peers)])
    kept = pl.pallas_call(
        functools.partial(keep_kernel, **settings),
        in_specs=[smem, vmem, vmem, vmem],
        out_specs=vmem,
        out_shape=pltpu.VMEM((half * tree, width), jnp.float32),
        scratch_shapes=working,
        compiler_params=limit,
        name="keep_part",
    )(
        pltpu.with_memory_space_constraint(known, pltpu.MemorySpace.SMEM),
        here(kept_query), here(kept_keys), here(kept_values),
    )
    return kept, arrived, own


def join_kernel(mine, other, out, *, heads, size, order):
    count = mine.shape[0]
    width = heads * size
    each = out.shape[1]

    def put(value, lane_slice):
        value = value.astype(out.dtype)
        for i, first in enumerate(order):
            out[i, :, lane_slice] = value[first : first + each]

    a, b = mine[:, width:].astype(jnp.float32), other[:, width:].astype(jnp.float32)
    lane = iota((count, lanes), 1)
    top = jnp.maximum(a, b)
    fa = jnp.where(lane < heads, jnp.exp2(a - top), 0.0)
    fb = jnp.where(lane < heads, jnp.exp2(b - top), 0.0)
    high = a * pltpu.roll(fa, heads, 1) + b * pltpu.roll(fb, heads, 1)
    low = a * pltpu.roll(fa, 2 * heads, 1) + b * pltpu.roll(fb, 2 * heads, 1)
    total = high + pltpu.roll(low, lanes - heads, 1)
    high = total.astype(jnp.bfloat16).astype(jnp.float32)
    low = pltpu.roll(total - high, heads, 1)
    stats = jnp.where(lane < heads, top, jnp.where(lane < 2 * heads, high, low))
    put(stats, slice(width, width + lanes))
    for h in range(heads):
        part = slice(h * size, (h + 1) * size)
        sum_ = mine[:, part].astype(jnp.float32) * fa[:, h : h + 1]
        sum_ = sum_ + other[:, part].astype(jnp.float32) * fb[:, h : h + 1]
        put(sum_, part)


def local_call(kernel, shape, dtype, *arrays):
    vmem = pl.BlockSpec(memory_space=pltpu.VMEM)
    return pl.pallas_call(
        kernel,
        in_specs=[vmem] * len(arrays),
        out_specs=vmem,
        out_shape=pltpu.VMEM(shape, dtype),
        compiler_params=pltpu.CompilerParams(vmem_limit_bytes=16 << 20),
    )(*(here(a) for a in arrays))


def finish_kernel(parts, own, out, *, heads, size):
    peers, count, _ = parts.shape
    width = heads * size
    lane = iota((count, lanes), 1)
    stats = [parts[p, :, width:].astype(jnp.float32) for p in range(peers)] + [own[:, width:]]
    top = stats[0]
    for s in stats[1:]:
        top = jnp.maximum(top, s)
    factors = [jnp.where(lane < heads, jnp.exp2(s - top), 0.0) for s in stats]
    high, low = jnp.zeros_like(top), jnp.zeros_like(top)
    for s, f in zip(stats, factors):
        high = high + s * pltpu.roll(f, heads, 1)
        low = low + s * pltpu.roll(f, 2 * heads, 1)
    total = pltpu.roll(high, lanes - heads, 1) + pltpu.roll(low, lanes - 2 * heads, 1)
    inverse = 1.0 / jnp.where(lane < heads, total, 1.0)
    for h in range(heads):
        part = slice(h * size, (h + 1) * size)
        merged = own[:, part] * factors[peers][:, h : h + 1]
        for p in range(peers):
            merged = merged + parts[p, :, part].astype(jnp.float32) * factors[p][:, h : h + 1]
        row = (merged * inverse[:, h : h + 1]).astype(out.dtype)
        for p in range(out.shape[0]):
            out[p, :, part] = row


def project_kernel(mine, other, weight, next_weight, out, *, head_peers, block_order):
    place = lax.axis_index("seq")
    core, y = lax.rem(place, 2), lax.div(place, lax.axis_size("seq") // 2)
    blocks = head_peers // 2
    rows = out.shape[1]
    for array, half in ((mine, core), (other, 1 - core)):
        for columns, at in ((weight, y), (next_weight, 1 - y)):
            part = f32dot(array[...], columns[...]).astype(out.dtype)
            last = at * head_peers + head_peers - 1 - half * blocks
            for k, b in enumerate(block_order):
                out[last - b] = part[k * rows : (k + 1) * rows]


def body(queries, new_keys, new_values, cache_keys, cache_values, parents, kv_lengths, out_weight):
    requests, tree, heads, size = queries.shape
    peers = lax.axis_size("seq")
    head_peers = lax.axis_size("head")
    tokens = requests * tree
    block = cache_keys.shape[1]
    chips, line = peers // 2, peers // 4
    count = tokens // peers
    width = heads * size
    rows = tokens // head_peers
    scale = math.log2(math.e) / math.sqrt(size)
    per = rows // 2 // count
    line_order = [*range(line // 2, line), *range(line // 2)]
    chip_order = [(y, z) for y in (1, 0) for z in line_order]
    plane_order = [(y, h) for y in range(2) for h in reversed(range(head_peers))]
    same_core = [[2 * (y * line + z) + c for y, z in chip_order] for c in range(2)]
    same_line = [[2 * (y * line + z) + c for z in line_order] for y in range(2) for c in range(2)]
    same_plane = [
        [(2 * (y * line + z) + c) * head_peers + h for y, h in plane_order]
        for z in range(line) for c in range(2)
    ]
    order = [z // per * rows + y * (rows // 2) + z % per * count for y, z in chip_order]
    block_order = [z // per for z in line_order[::per]]
    query_rows = queries.reshape(requests, tree * heads, size)
    kept, arrived, own = cache_parts(
        kv_lengths, parents, query_rows,
        new_keys.reshape(requests, tree, size), new_values.reshape(requests, tree, size),
        cache_keys.reshape(requests, block, size), cache_values.reshape(requests, block, size),
        heads, peers, head_peers, scale,
    )
    next_weight = lax.ppermute(out_weight, "seq", [(i, (i + chips) % peers) for i in range(peers)])
    pair = local_call(
        functools.partial(join_kernel, heads=heads, size=size, order=order),
        (chips, count, width + lanes), jnp.bfloat16, kept, arrived,
    )
    parts = lax.all_to_all(pair, "seq", 0, 0, tiled=True, axis_index_groups=same_core)
    share = local_call(
        functools.partial(finish_kernel, heads=heads, size=size),
        (line, count, width), jnp.bfloat16, parts, own,
    )
    mine = lax.all_to_all(share, "seq", 0, 0, tiled=True, axis_index_groups=same_line)
    mine = mine.reshape(line * count, width)
    other = lax.ppermute(mine, "seq", [(i, i ^ 1) for i in range(peers)])
    partial = local_call(
        functools.partial(project_kernel, head_peers=head_peers, block_order=block_order),
        (2 * head_peers, rows // 2, out_weight.shape[1]), jnp.bfloat16,
        mine, other, out_weight, next_weight,
    )
    pieces = lax.all_to_all(partial, ("seq", "head"), 0, 0, tiled=True, axis_index_groups=same_plane)
    pieces = pieces.reshape(2, head_peers, rows // 2, -1).astype(jnp.float32).sum(axis=1)
    return pieces.reshape(rows, -1).astype(jnp.bfloat16)


def solution(mesh):
    placed = (
        P(None, None, "head", None),
        P(None, None, "head", None),
        P(None, None, "head", None),
        P(None, "seq", "head", None),
        P(None, "seq", "head", None),
        P(),
        P(),
        P("head", "seq"),
    )

    return jax.shard_map(body, mesh=mesh, in_specs=placed, out_specs=P("head", "seq"), check_vma=False)
```

time: 61.6 us -> 54.8 us (0.89)
  blocking collectives: 25.8 us -> 20.2 us
  Pallas kernels: 12.4 us -> 10.2 us
  waiting for transfers between devices: 7.23 us -> 8.61 us
    all_to_all x1, blocking collectives: 13.3 us -> 10.5 us  [body(): lax.all_to_all(partial, ('seq', 'head'), 0, 0, tiled=True, axis_index_gro...]
    all_to_all x1, blocking collectives: 12.5 us -> 9.74 us  [body(): lax.all_to_all(share, 'seq', 0, 0, tiled=True, axis_index_groups=same_line)]
    pallas_call x3 -> x2, Pallas kernels: 10.4 us -> 8.23 us  [the longest x1 5.31 us: cache_parts(): pl.pallas_call(functools.partial(send_kernel, peers=peers, head_peers=hea...]
    all_to_all x1, starting transfers between devices: 7.6 us -> 9.63 us  [body(): lax.all_to_all(pair, 'seq', 0, 0, tiled=True, axis_index_groups=same_core)]
    all_to_all x1, waiting for transfers between devices: 6.24 us -> 7.62 us  [body(): lax.all_to_all(pair, 'seq', 0, 0, tiled=True, axis_index_groups=same_core)]
    ppermute x1, starting transfers between devices: 2.78 us -> 1.64 us  [body(): other = lax.ppermute(mine, 'seq', [(i, i ^ 1) for i in range(peers)])]
    ppermute x1, starting transfers between devices: 1.45 us -> 0.32 us  [body(): lax.ppermute(out_weight, 'seq', [(i, (i + chips) % peers) for i in range(...]
  transfers between devices with their start and end apart: 4 -> 4, of which waited for: 2 -> 2; matrix products, arithmetic and copies ran while one was open for 0% -> 0% of each run, Pallas kernels for 9% -> 6%
where the time goes in v4:
time: 54.8 us; the launch traced here: 54.6 us
  blocking collectives  20.2 us (37%)
  starting transfers between devices  14.9 us (27%)
  Pallas kernels  10.2 us (19%)
  waiting for transfers between devices  8.61 us (16%)
  other arithmetic  0.63 us (1%)
    all_to_all x1, blocking collectives, body(): lax.all_to_all(partial, ('seq', 'head'), 0, 0, tiled=True, axis_index_gro...  10.5 us
    all_to_all x1, blocking collectives, body(): lax.all_to_all(share, 'seq', 0, 0, tiled=True, axis_index_groups=same_line)  9.74 us
    all_to_all x1, starting transfers between devices, body(): lax.all_to_all(pair, 'seq', 0, 0, tiled=True, axis_index_groups=same_core)  9.63 us
    all_to_all x1, waiting for transfers between devices, body(): lax.all_to_all(pair, 'seq', 0, 0, tiled=True, axis_index_groups=same_core)  7.62 us
    pallas_call x1, Pallas kernels, cache_parts(): pl.pallas_call(functools.partial(send_kernel, peers=peers, head_peers=hea...  5.31 us
    ppermute x1, starting transfers between devices, cache_parts(): arrived = lax.ppermute(sent, 'seq', [(i, i ^ 1) for i in range(peers)])  3.28 us
    pallas_call x1, Pallas kernels, cache_parts(): pl.pallas_call(functools.partial(keep_kernel, **settings), in_specs=[smem...  2.92 us
    pallas_call x3, Pallas kernels, local_call(): pl.pallas_call(kernel, in_specs=[vmem] * len(arrays), out_specs=vmem, out...  2 us
  transfers between devices with their start and end apart: 4, of which 2 were waited for; matrix products, arithmetic and copies ran while one was open for 0% of the time, Pallas kernels for 6%

profile of v4, /device:TPU:1, one launch (start us, length us, event | category | flops | bytes accessed | tf_op | source)
XLA Modules:
  0.0 54.6 jit_solution(2639354175228614909)
XLA Ops:
  0.0 5.3 %send_part.1 = (bf16[128,1152]{1,0:T(8,128)(2,1)S(1)}, f32[8,1152]{1,0:T(8,128)S(1)}, s32[4]{0:T(128)S(4)}, bf16[2,512,128]{2,1,0:T(8,128)(2,1)S(1)}, bf16[2,204...) custom-call(s32[4]{0:T(128)} %lengths_far.1, s32[4,64]{1,0:T(4,128)} %parents_far.1, ...), custom_call_target="tpu_custom_call" | custom-call | tf_op jit(solution)/shard_map/send_part/pallas_call | solution.py:226
  5.3 3.3 %collective-permute-start = (bf16[128,1152]{1,0:T(8,128)(2,1)S(1)}, bf16[128,1152]{1,0:T(8,128)(2,1)S(1)}, u32[]{:S(2)}, u32[]{:S(2)}) collective-permute-start(bf16[128,1152]{1,0:T(8,128)(2,1)S(1)} %get-tuple-element.15), channel_id=1, source_target_pairs={{0,8},{8,0},{16,24},{24,16},{32,40},{40,32},{48,56},{56,48},{64,72... | collective-permute-start | bytes 884744 | tf_op jit(solution)/shard_map/ppermute | solution.py:253
  8.6 0.0 copy-start
  8.6 2.9 %keep_part.1.mine = f32[128,1152]{1,0:T(8,128)S(1)} custom-call(s32[4]{0:T(128)S(4)} %get-tuple-element.11.lengths, bf16[2,512,128]{2,1,0:T(8,128)(2,1)S(1)} %get-tuple-element.12.query, bf16[2,2048,128]{2,1,0:T(8,128)(2,1)S(1)} %get-tuple-element.13.keys, bf16[2,2048,128]{2,1,0:T(8,128)(2,1)S(1)} %get-tuple-element.14.values), custom_call_target="tpu_custom_call" | custom-call | tf_op jit(solution)/shard_map/keep_part/pallas_call | solution.py:254
  11.5 0.0 collective-permute-done.other
  11.5 1.2 %shard_map.82 = bf16[16,8,1152]{2,1,0:T(8,128)(2,1)} custom-call(f32[128,1152]{1,0:T(8,128)S(1)} %keep_part.1.mine, bf16[128,1152]{1,0:T(8,128)(2,1)S(1)} %collective-permute-done.other), custom_call_target="tpu_custom_call" | custom-call | tf_op jit(solution)/shard_map/pallas_call | solution.py:300
  12.8 9.6 %all-to-all-start = ((bf16[16,8,1152]{2,1,0:T(8,128)(2,1)}), bf16[16,8,1152]{2,1,0:T(8,128)(2,1)S(1)}, u32[]{:S(2)}, u32[]{:S(2)}) async-start(bf16[16,8,1152]{2,1,0:T(8,128)(2,1)} %shard_map.82), calls=%async_computation | async-start | bytes 589824 | tf_op jit(solution)/shard_map/all_to_all | solution.py:382
  22.4 0.0 copy-done
  22.4 0.3 collective-permute-start.2
  22.7 7.6 %all-to-all-done.parts = bf16[16,8,1152]{2,1,0:T(8,128)(2,1)S(1)} async-done(((bf16[16,8,1152]{2,1,0:T(8,128)(2,1)}), bf16[16,8,1152]{2,1,0:T(8,128)(2,1)S(1)}, u32[]{:S(2)}, u32[]{:S(2)}) %all-to-all-start) | async-done | bytes 294944 | tf_op jit(solution)/shard_map/all_to_all | solution.py:382
  30.3 0.3 shard_map.83
  30.7 9.7 %all_to_all.15 = bf16[8,8,1024]{2,1,0:T(8,128)(2,1)S(1)} all-to-all(bf16[8,8,1024]{2,1,0:T(8,128)(2,1)S(1)} %shard_map.83), channel_id=1, replica_groups={{64,80,96,112,0,16,32,48},{72,88,104,120,8,24,40,56},{192,208,224,240,1..., dimensions={0} | all-to-all | bytes 262144 | tf_op jit(solution)/shard_map/all_to_all | solution.py:387
  40.4 1.6 %collective-permute-start.1 = (bf16[64,1024]{1,0:T(8,128)(2,1)S(1)}, bf16[64,1024]{1,0:T(8,128)(2,1)S(1)}, u32[]{:S(2)}, u32[]{:S(2)}) collective-permute-start(bf16[64,1024]{1,0:T(8,128)(2,1)S(1)} %bitcast.9), channel_id=1, source_target_pairs={{0,8},{8,0},{16,24},{24,16},{32,40},{40,32},{48,56},{56,48},{64,72... | collective-permute-start | bytes 393224 | tf_op jit(solution)/shard_map/ppermute | solution.py:389
  42.0 0.0 collective-permute-done.2.next_weight
  42.0 1.0 %collective-permute-done.1.other = bf16[64,1024]{1,0:T(8,128)(2,1)S(1)} collective-permute-done((bf16[64,1024]{1,0:T(8,128)(2,1)S(1)}, bf16[64,1024]{1,0:T(8,128)(2,1)S(1)}, u32[]{:S(2)}, u32[]{:S(2)}) %collective-permute-start.1) | collective-permute-done | bytes 131104 | tf_op jit(solution)/shard_map/ppermute | solution.py:389
  43.0 0.5 shard_map.84
  43.5 10.5 %all_to_all.16 = bf16[16,16,256]{2,1,0:T(8,128)(2,1)S(1)} all-to-all(bf16[16,16,256]{2,1,0:T(8,128)(2,1)S(1)} %shard_map.84), channel_id=1, replica_groups={{7,6,5,4,3,2,1,0,135,134,133,132,131,130,129,128},{15,14,13,12,11,10,9,..., dimensions={0} | all-to-all | bytes 262144 | tf_op jit(solution)/shard_map/all_to_all | solution.py:395
  54.0 0.6 %bitcast_reduce_fusion = bf16[2,16,256]{2,1,0:T(8,128)(2,1)} fusion(bf16[16,16,256]{2,1,0:T(8,128)(2,1)S(1)} %all_to_all.16), kind=kLoop, calls=%fused_computation | loop fusion | flops 57344 | bytes 147456 | tf_op jit(solution)/shard_map/reduce_sum | solution.py:396
Async XLA Ops:
  5.3 6.2 %collective-permute-start = (bf16[128,1152]{1,0:T(8,128)(2,1)S(1)}, bf16[128,1152]{1,0:T(8,128)(2,1)S(1)}, u32[]{:S(2)}, u32[]{:S(2)}) collective-permute-start(bf16[128,1152]{1,0:T(8,128)(2,1)S(1)} %get-tuple-element.15), channel_id=1, source_target_pairs={{0,8},{8,0},{16,24},{24,16},{32,40},{40,32},{48,56},{56,48},{64,72... | collective-permute-start | bytes 884744 | tf_op jit(solution)/shard_map/ppermute | solution.py:253
  8.6 13.8 %copy-start = (bf16[1024,256]{1,0:T(8,128)(2,1)S(1)}, bf16[1024,256]{1,0:T(8,128)(2,1)}, u32[]{:S(2)}) copy-start(bf16[1024,256]{1,0:T(8,128)(2,1)} %weight.1) | copy-start | bytes 1572868
  12.8 17.6 %all-to-all-start = ((bf16[16,8,1152]{2,1,0:T(8,128)(2,1)}), bf16[16,8,1152]{2,1,0:T(8,128)(2,1)S(1)}, u32[]{:S(2)}, u32[]{:S(2)}) async-start(bf16[16,8,1152]{2,1,0:T(8,128)(2,1)} %shard_map.82), calls=%async_computation | async-start | bytes 589824 | tf_op jit(solution)/shard_map/all_to_all | solution.py:382
  22.4 19.6 %collective-permute-start.2 = (bf16[1024,256]{1,0:T(8,128)(2,1)S(1)}, bf16[1024,256]{1,0:T(8,128)(2,1)S(1)}, u32[]{:S(2)}, u32[]{:S(2)}) collective-permute-start(bf16[1024,256]{1,0:T(8,128)(2,1)S(1)} %copy-done), channel_id=1, source_target_pairs={{0,128},{8,136},{16,144},{24,152},{32,160},{40,168},{48,176},{56,1... | collective-permute-start | bytes 1572872 | tf_op jit(solution)/shard_map/ppermute | solution.py:377
  40.4 2.6 %collective-permute-start.1 = (bf16[64,1024]{1,0:T(8,128)(2,1)S(1)}, bf16[64,1024]{1,0:T(8,128)(2,1)S(1)}, u32[]{:S(2)}, u32[]{:S(2)}) collective-permute-start(bf16[64,1024]{1,0:T(8,128)(2,1)S(1)} %bitcast.9), channel_id=1, source_target_pairs={{0,8},{8,0},{16,24},{24,16},{32,40},{40,32},{48,56},{56,48},{64,72... | collective-permute-start | bytes 393224 | tf_op jit(solution)/shard_map/ppermute | solution.py:389

commit v5 on v4

--- a/solution.py
+++ b/solution.py
@@ -109,7 +109,7 @@
 
 
 def attend(
-    query, keys, values, valids, out, scratch, tree, heads, scale, chunk, beside=None
+    query, keys, values, valids, out, scratch, tree, heads, scale, chunk, beside=None, after=None
 ):
     scores, *partial = scratch
     number = query.shape[0]
@@ -118,6 +118,8 @@
         if r == number - 1 and beside is not None:
             beside()
         tops.append(score(query.at[r], keys.at[r], valids[r], scores.at[r], scale, chunk))
+    if after is not None:
+        after()
     for r in range(number):
         gather_values(scores.at[r], values.at[r], tops[r], [a.at[r] for a in partial], scale, chunk)
     for r in range(number):
@@ -125,17 +127,22 @@
         store_partial(top, out.at[pl.ds(r * tree, tree)], [a.at[r] for a in partial], heads, valids[r] > 0)
 
 
-def draft(query, keys, values, parent_row, first, out, partial, heads, scale):
-    rows, size = query.shape
-    tree = keys.shape[0]
-    count = rows // heads
-    acc, sums, _ = partial
+def ancestors(parent_row, first, count):
+    tree = parent_row.shape[1]
     j, i = iota((tree, tree), 0), iota((tree, tree), 1)
     reached = ((parent_row == j) | (i == j)).astype(jnp.bfloat16)
     for _ in range(max(1, (tree - 1).bit_length())):
         reached = jnp.minimum(f32dot(reached, reached), 1.0).astype(jnp.bfloat16)
     own = iota((count, tree), 1) == iota((count, tree), 0) + first
-    allowed = f32dot(own.astype(jnp.bfloat16), reached, dims_last) > 0.5
+    return f32dot(own.astype(jnp.bfloat16), reached, dims_last)
+
+
+def draft(query, keys, values, seen, out, partial, heads, scale):
+    rows, size = query.shape
+    tree = keys.shape[0]
+    count = rows // heads
+    acc, sums, _ = partial
+    allowed = seen > 0.5
     s = f32dot(query[...], keys[...], dims_last).reshape(count, heads, tree)
     s = jnp.where(allowed[:, None, :], s * scale, lowest).reshape(rows, tree)
     top = jnp.max(s, axis=1, keepdims=True)
@@ -164,8 +171,9 @@
     request, first = owned(place, requests, tree, peers, head_peers)
     own_first = pl.multiple_of(first * heads, own_rows)
 
-    pairs = [(lengths_far, lengths), (queries.at[pl.ds(left, half)], query)]
-    pairs += [(keys.at[left], left_keys.at[0]), (parents_far, parents)]
+    pairs = [(parents_far, parents), (lengths_far, lengths)]
+    pairs += [(queries.at[pl.ds(left, half)], query), (keys.at[left], left_keys.at[0])]
+    early = len(pairs)
     pairs += [(queries.at[request, pl.ds(own_first, own_rows)], own_query)]
     pairs += [(draft_keys.at[request], tree_keys), (draft_values.at[request], tree_values)]
     pairs += [(keys.at[left + r], left_keys.at[r]) for r in range(1, half)]
@@ -174,24 +182,28 @@
     pairs += [(queries.at[pl.ds(mine, half)], kept_query)]
     pairs += [(keys.at[pl.ds(mine, half)], kept_keys), (values.at[pl.ds(mine, half)], kept_values)]
     copies = [pltpu.make_async_copy(a, b, sems.at[i]) for i, (a, b) in enumerate(pairs)]
-    for copy in copies:
+    for copy in copies[:late]:
         copy.start()
-    early = 3
-    for copy in copies[:early]:
+    copies[0].wait()
+    seen = ancestors(parents[pl.ds(request, 1), :], first, own_rows // heads)
+    for copy in copies[1:early]:
         copy.wait()
+    for copy in copies[late:]:
+        copy.start()
 
     def rest():
-        for copy in copies[early:late]:
+        for copy in copies[early : late - half]:
             copy.wait()
-        draft(
-            own_query, tree_keys, tree_values, parents[pl.ds(request, 1), :], first, own,
-            (own_acc, own_sums, own_peak), heads, scale,
-        )
+
+    def last():
+        for copy in copies[late - half : late]:
+            copy.wait()
+        draft(own_query, tree_keys, tree_values, seen, own, (own_acc, own_sums, own_peak), heads, scale)
 
     attend(
         query, left_keys, left_values, [lengths[left + r] - place * block for r in range(half)],
         sent, (scores, acc, sums, peak), tree, heads, scale, chunk,
-        rest,
+        rest, last,
     )
     for copy in copies[late:]:
         copy.wait()
@@ -357,7 +369,7 @@
     scale = math.log2(math.e) / math.sqrt(size)
     per = rows // 2 // count
     line_order = [*range(line // 2, line), *range(line // 2)]
-    chip_order = [(y, z) for y in (1, 0) for z in line_order]
+    chip_order = [(y, z) for y in range(2) for z in line_order]
     plane_order = [(y, h) for y in range(2) for h in reversed(range(head_peers))]
     same_core = [[2 * (y * line + z) + c for y, z in chip_order] for c in range(2)]
     same_line = [[2 * (y * line + z) + c for z in line_order] for y in range(2) for c in range(2)]

time: 54.8 us -> 54.4 us (level)
  starting transfers between devices: 14.9 us -> 16.2 us
  waiting for transfers between devices: 8.61 us -> 7.5 us
    all_to_all x1, waiting for transfers between devices: 7.62 us -> 6.51 us  [body(): lax.all_to_all(pair, 'seq', 0, 0, tiled=True, axis_index_groups=same_core)]
    ppermute x1, starting transfers between devices: 0.32 us -> 1.27 us  [body(): lax.ppermute(out_weight, 'seq', [(i, (i + chips) % peers) for i in range(...]
    ppermute x1, starting transfers between devices: 1.64 us -> 2.46 us  [body(): other = lax.ppermute(mine, 'seq', [(i, i ^ 1) for i in range(peers)])]
where the time goes in v5:
time: 54.4 us; the launch traced here: 54.1 us
  blocking collectives  19.8 us (36%)
  starting transfers between devices  16.2 us (30%)
  Pallas kernels  9.96 us (18%)
  waiting for transfers between devices  7.5 us (14%)
  other arithmetic  0.63 us (1%)
    all_to_all x1, blocking collectives, body(): lax.all_to_all(partial, ('seq', 'head'), 0, 0, tiled=True, axis_index_gro...  10.2 us
    all_to_all x1, blocking collectives, body(): lax.all_to_all(share, 'seq', 0, 0, tiled=True, axis_index_groups=same_line)  9.58 us
    all_to_all x1, starting transfers between devices, body(): lax.all_to_all(pair, 'seq', 0, 0, tiled=True, axis_index_groups=same_core)  9.16 us
    all_to_all x1, waiting for transfers between devices, body(): lax.all_to_all(pair, 'seq', 0, 0, tiled=True, axis_index_groups=same_core)  6.51 us
    pallas_call x1, Pallas kernels, cache_parts(): pl.pallas_call(functools.partial(send_kernel, peers=peers, head_peers=hea...  5.03 us
    ppermute x1, starting transfers between devices, cache_parts(): arrived = lax.ppermute(sent, 'seq', [(i, i ^ 1) for i in range(peers)])  3.29 us
    pallas_call x1, Pallas kernels, cache_parts(): pl.pallas_call(functools.partial(keep_kernel, **settings), in_specs=[smem...  2.92 us
    ppermute x1, starting transfers between devices, body(): other = lax.ppermute(mine, 'seq', [(i, i ^ 1) for i in range(peers)])  2.46 us
  transfers between devices with their start and end apart: 4, of which 2 were waited for; matrix products, arithmetic and copies ran while one was open for 0% of the time, Pallas kernels for 6%

profile of v5, /device:TPU:1, one launch (start us, length us, event | category | flops | bytes accessed | tf_op | source)
XLA Modules:
  0.0 54.1 jit_solution(18044705145923836457)
XLA Ops:
  0.0 5.0 %send_part.1 = (bf16[128,1152]{1,0:T(8,128)(2,1)S(1)}, f32[8,1152]{1,0:T(8,128)S(1)}, s32[4]{0:T(128)S(4)}, bf16[2,512,128]{2,1,0:T(8,128)(2,1)S(1)}, bf16[2,204...) custom-call(s32[4]{0:T(128)} %lengths_far.1, s32[4,64]{1,0:T(4,128)} %parents_far.1, ...), custom_call_target="tpu_custom_call" | custom-call | tf_op jit(solution)/shard_map/send_part/pallas_call | solution.py:238
  5.0 3.3 %collective-permute-start = (bf16[128,1152]{1,0:T(8,128)(2,1)S(1)}, bf16[128,1152]{1,0:T(8,128)(2,1)S(1)}, u32[]{:S(2)}, u32[]{:S(2)}) collective-permute-start(bf16[128,1152]{1,0:T(8,128)(2,1)S(1)} %get-tuple-element.15), channel_id=1, source_target_pairs={{0,8},{8,0},{16,24},{24,16},{32,40},{40,32},{48,56},{56,48},{64,72... | collective-permute-start | bytes 884744 | tf_op jit(solution)/shard_map/ppermute | solution.py:265
  8.3 0.0 copy-start
  8.3 2.9 %keep_part.1.mine = f32[128,1152]{1,0:T(8,128)S(1)} custom-call(s32[4]{0:T(128)S(4)} %get-tuple-element.11.lengths, bf16[2,512,128]{2,1,0:T(8,128)(2,1)S(1)} %get-tuple-element.12.query, bf16[2,2048,128]{2,1,0:T(8,128)(2,1)S(1)} %get-tuple-element.13.keys, bf16[2,2048,128]{2,1,0:T(8,128)(2,1)S(1)} %get-tuple-element.14.values), custom_call_target="tpu_custom_call" | custom-call | tf_op jit(solution)/shard_map/keep_part/pallas_call | solution.py:266
  11.3 0.0 collective-permute-done.other
  11.3 1.2 %shard_map.82 = bf16[16,8,1152]{2,1,0:T(8,128)(2,1)} custom-call(f32[128,1152]{1,0:T(8,128)S(1)} %keep_part.1.mine, bf16[128,1152]{1,0:T(8,128)(2,1)S(1)} %collective-permute-done.other), custom_call_target="tpu_custom_call" | custom-call | tf_op jit(solution)/shard_map/pallas_call | solution.py:312
  12.5 9.2 %all-to-all-start = ((bf16[16,8,1152]{2,1,0:T(8,128)(2,1)}), bf16[16,8,1152]{2,1,0:T(8,128)(2,1)S(1)}, u32[]{:S(2)}, u32[]{:S(2)}) async-start(bf16[16,8,1152]{2,1,0:T(8,128)(2,1)} %shard_map.82), calls=%async_computation | async-start | bytes 589824 | tf_op jit(solution)/shard_map/all_to_all | solution.py:394
  21.7 0.0 copy-done
  21.7 1.3 %collective-permute-start.2 = (bf16[1024,256]{1,0:T(8,128)(2,1)S(1)}, bf16[1024,256]{1,0:T(8,128)(2,1)S(1)}, u32[]{:S(2)}, u32[]{:S(2)}) collective-permute-start(bf16[1024,256]{1,0:T(8,128)(2,1)S(1)} %copy-done), channel_id=1, source_target_pairs={{0,128},{8,136},{16,144},{24,152},{32,160},{40,168},{48,176},{56,1... | collective-permute-start | bytes 1572872 | tf_op jit(solution)/shard_map/ppermute | solution.py:389
  22.9 6.5 %all-to-all-done.parts = bf16[16,8,1152]{2,1,0:T(8,128)(2,1)S(1)} async-done(((bf16[16,8,1152]{2,1,0:T(8,128)(2,1)}), bf16[16,8,1152]{2,1,0:T(8,128)(2,1)S(1)}, u32[]{:S(2)}, u32[]{:S(2)}) %all-to-all-start) | async-done | bytes 294944 | tf_op jit(solution)/shard_map/all_to_all | solution.py:394
  29.5 0.3 shard_map.83
  29.8 9.6 %all_to_all.15 = bf16[8,8,1024]{2,1,0:T(8,128)(2,1)S(1)} all-to-all(bf16[8,8,1024]{2,1,0:T(8,128)(2,1)S(1)} %shard_map.83), channel_id=1, replica_groups={{64,80,96,112,0,16,32,48},{72,88,104,120,8,24,40,56},{192,208,224,240,1..., dimensions={0} | all-to-all | bytes 262144 | tf_op jit(solution)/shard_map/all_to_all | solution.py:399
  39.3 2.5 %collective-permute-start.1 = (bf16[64,1024]{1,0:T(8,128)(2,1)S(1)}, bf16[64,1024]{1,0:T(8,128)(2,1)S(1)}, u32[]{:S(2)}, u32[]{:S(2)}) collective-permute-start(bf16[64,1024]{1,0:T(8,128)(2,1)S(1)} %bitcast.9), channel_id=1, source_target_pairs={{0,8},{8,0},{16,24},{24,16},{32,40},{40,32},{48,56},{56,48},{64,72... | collective-permute-start | bytes 393224 | tf_op jit(solution)/shard_map/ppermute | solution.py:401
  41.8 0.0 collective-permute-done.2.next_weight
  41.8 1.0 %collective-permute-done.1.other = bf16[64,1024]{1,0:T(8,128)(2,1)S(1)} collective-permute-done((bf16[64,1024]{1,0:T(8,128)(2,1)S(1)}, bf16[64,1024]{1,0:T(8,128)(2,1)S(1)}, u32[]{:S(2)}, u32[]{:S(2)}) %collective-permute-start.1) | collective-permute-done | bytes 131104 | tf_op jit(solution)/shard_map/ppermute | solution.py:401
  42.8 0.5 shard_map.84
  43.3 10.2 %all_to_all.16 = bf16[16,16,256]{2,1,0:T(8,128)(2,1)S(1)} all-to-all(bf16[16,16,256]{2,1,0:T(8,128)(2,1)S(1)} %shard_map.84), channel_id=1, replica_groups={{7,6,5,4,3,2,1,0,135,134,133,132,131,130,129,128},{15,14,13,12,11,10,9,..., dimensions={0} | all-to-all | bytes 262144 | tf_op jit(solution)/shard_map/all_to_all | solution.py:407
  53.5 0.6 %bitcast_reduce_fusion = bf16[2,16,256]{2,1,0:T(8,128)(2,1)} fusion(bf16[16,16,256]{2,1,0:T(8,128)(2,1)S(1)} %all_to_all.16), kind=kLoop, calls=%fused_computation | loop fusion | flops 57344 | bytes 147456 | tf_op jit(solution)/shard_map/reduce_sum | solution.py:408
Async XLA Ops:
  5.0 6.2 %collective-permute-start = (bf16[128,1152]{1,0:T(8,128)(2,1)S(1)}, bf16[128,1152]{1,0:T(8,128)(2,1)S(1)}, u32[]{:S(2)}, u32[]{:S(2)}) collective-permute-start(bf16[128,1152]{1,0:T(8,128)(2,1)S(1)} %get-tuple-element.15), channel_id=1, source_target_pairs={{0,8},{8,0},{16,24},{24,16},{32,40},{40,32},{48,56},{56,48},{64,72... | collective-permute-start | bytes 884744 | tf_op jit(solution)/shard_map/ppermute | solution.py:265
  8.3 13.3 %copy-start = (bf16[1024,256]{1,0:T(8,128)(2,1)S(1)}, bf16[1024,256]{1,0:T(8,128)(2,1)}, u32[]{:S(2)}) copy-start(bf16[1024,256]{1,0:T(8,128)(2,1)} %weight.1) | copy-start | bytes 1572868
  12.5 17.0 %all-to-all-start = ((bf16[16,8,1152]{2,1,0:T(8,128)(2,1)}), bf16[16,8,1152]{2,1,0:T(8,128)(2,1)S(1)}, u32[]{:S(2)}, u32[]{:S(2)}) async-start(bf16[16,8,1152]{2,1,0:T(8,128)(2,1)} %shard_map.82), calls=%async_computation | async-start | bytes 589824 | tf_op jit(solution)/shard_map/all_to_all | solution.py:394
  21.7 20.1 %collective-permute-start.2 = (bf16[1024,256]{1,0:T(8,128)(2,1)S(1)}, bf16[1024,256]{1,0:T(8,128)(2,1)S(1)}, u32[]{:S(2)}, u32[]{:S(2)}) collective-permute-start(bf16[1024,256]{1,0:T(8,128)(2,1)S(1)} %copy-done), channel_id=1, source_target_pairs={{0,128},{8,136},{16,144},{24,152},{32,160},{40,168},{48,176},{56,1... | collective-permute-start | bytes 1572872 | tf_op jit(solution)/shard_map/ppermute | solution.py:389
  39.3 3.5 %collective-permute-start.1 = (bf16[64,1024]{1,0:T(8,128)(2,1)S(1)}, bf16[64,1024]{1,0:T(8,128)(2,1)S(1)}, u32[]{:S(2)}, u32[]{:S(2)}) collective-permute-start(bf16[64,1024]{1,0:T(8,128)(2,1)S(1)} %bitcast.9), channel_id=1, source_target_pairs={{0,8},{8,0},{16,24},{24,16},{32,40},{40,32},{48,56},{56,48},{64,72... | collective-permute-start | bytes 393224 | tf_op jit(solution)/shard_map/ppermute | solution.py:401
